TPU v7x, 512 devices: a whole 4x8x8 slice. The times are simulated.
512 devices in a mesh: seq: 128 (over y, z, core), head: 4 (over x).
Axes of the slice: x: 4, y: 8, z: 8, core: 2. Of those that a mesh axis runs over, the one named last changes fastest.
Arguments:
- hidden_states: bfloat16 [8, 8192, 3584], P(None, 'seq', 'head'), may hold values from -6 to 6
- boundary: int32 [8, 64], replicated, may hold values from 0 to 8191, as said below
- valid: int32 [8, 64], replicated, may hold values from 0 to 1, as said below
- pairs: int32 [8, 2], replicated, may hold values from 0 to 7, as said below
- w_first: bfloat16 [3584, 4096], P('seq', 'head'), may hold values from -0.09375 to 0.09375
- b_first: float32 [4096], P('head'), may hold values from -3 to 3
- w_second: float32 [4096], P('head'), may hold values from -0.09375 to 0.09375
Outputs:
- step_reward: float32 [8, 64], replicated
- trace_score: float32 [8], replicated
- margin: float32 [8], replicated
Inputs may be any that keep to these rules, and one draw needn't show every extreme that they name: Within a trace the 64 boundary positions are distinct and increasing. In each trace the ones come first; every trace has 16 to 64 valid steps. `pairs`: the two traces of a pair differ.
All inputs are finite; a program needn't handle non-finite values.
Results may differ from a plain program's by a relative error of at most 0.0003.
Values may be sent and summed in bfloat16 or wider, within the bound.
No kernel may reach another device: no remote copies, remote signals or barrier semaphores. Data moves between devices by JAX's collectives and lax.ppermute only.
A program may use at most 64 MiB of HBM per device.

v0:
```python
import jax
import jax.numpy as jnp
from jax import lax
from jax.sharding import Mesh
from jax.sharding import PartitionSpec as P

SEQ = ("seq_0", "seq_1", "seq_2")
SEQ_HEAD = ("seq_0", "seq_1", "seq_2", "head")


def laid_out(pieces, dim):
    pieces = jnp.moveaxis(pieces, 0, dim)
    shape = pieces.shape
    return pieces.reshape(*shape[:dim], shape[dim] * shape[dim + 1], *shape[dim + 2 :])


def sent_to_all(shard, axis):
    copies = jnp.broadcast_to(shard, (lax.axis_size(axis), *shard.shape))
    return lax.all_to_all(copies, axis, split_axis=0, concat_axis=0, tiled=True)


def gather_directly(shard, axis, dim):
    return laid_out(sent_to_all(shard, axis), dim)


def over_axes(shard, axes):
    for axis in axes:
        shard = lax.psum(shard, axis)
    return shard


def score_rows(rows, w_first, b_first, w_second):
    pre = jnp.dot(
        rows, lax.all_gather(w_first, SEQ, axis=0, tiled=True), preferred_element_type=jnp.float32
    )
    return jnp.sum(jnp.maximum(pre + b_first, 0.0) * w_second, axis=-1)


def per_device(hidden_states, boundary, valid, pairs, w_first, b_first, w_second):
    traces, tok_dev, quarter = hidden_states.shape
    offset = lax.axis_index(SEQ) * tok_dev
    positions = offset + jnp.arange(tok_dev, dtype=jnp.int32)
    hits = boundary[:, :, None] == positions[None, None, :]
    whole = gather_directly(hidden_states, "head", 2)
    token_logit = score_rows(
        whole.reshape(traces * tok_dev, whole.shape[2]), w_first, b_first, w_second
    )
    token_logit = token_logit.reshape(traces, tok_dev)
    partial_logit = jnp.sum(jnp.where(hits, token_logit[:, None, :], 0.0), axis=2)
    logit = over_axes(partial_logit, SEQ_HEAD)
    live = valid == 1
    step_reward = jnp.where(live, logit, jnp.float32(0.0))
    trace_score = jnp.min(jnp.where(live, logit, jnp.float32(1e30)), axis=1)
    trace_ids = jnp.arange(traces, dtype=jnp.int32)[None, :]
    winner = jnp.sum(jnp.where(pairs[:, 0:1] == trace_ids, trace_score[None, :], 0.0), axis=1)
    loser = jnp.sum(jnp.where(pairs[:, 1:2] == trace_ids, trace_score[None, :], 0.0), axis=1)
    return (step_reward, trace_score, winner - loser)


def solution(mesh):
    torus = Mesh(
        mesh.devices.reshape(8, 8, 2, mesh.shape["head"]), ("seq_0", "seq_1", "seq_2", "head")
    )
    return jax.shard_map(
        per_device,
        mesh=torus,
        in_specs=(P(None, SEQ, "head"), P(), P(), P(), P(SEQ, "head"), P("head"), P("head")),
        out_specs=(P(), P(), P()),
        check_vma=False,
    )
```

profile of v0, /device:TPU:1, one launch (start us, length us, event | category | flops | bytes accessed | tf_op | source)
XLA Modules:
  0.0 175.0 jit_solution(17195538024517947789)
XLA Ops:
  7.2 0.0 all-gather.3.cloned.1.call-start
  7.2 0.7 all-gather.3.cloned.1.call-update
  7.9 3.6 %broadcast_in_dim.47 = bf16[4,8,64,896]{3,2,1,0:T(8,128)(2,1)} broadcast(bf16[8,64,896]{2,1,0:T(8,128)(2,1)} %param.7), dimensions={1,2,3} | broadcast | bytes 4587520 | tf_op jit(solution)/shard_map/broadcast_in_dim | solution.py:18
  11.5 0.0 copy-start.3
  11.5 5.0 %all-to-all-start = ((bf16[4,8,64,896]{3,2,1,0:T(8,128)(2,1)}), bf16[4,8,64,896]{3,2,1,0:T(8,128)(2,1)}, u32[]{:S(2)}, u32[]{:S(2)}) async-start(bf16[4,8,64,896]{3,2,1,0:T(8,128)(2,1)} %broadcast_in_dim.47), calls=%async_computation | async-start | bytes 7340032 | tf_op jit(solution)/shard_map/all_to_all | solution.py:19
  16.4 0.0 copy-done.3
  16.4 37.6 %all-to-all-done = bf16[4,8,64,896]{3,2,1,0:T(8,128)(2,1)} async-done(((bf16[4,8,64,896]{3,2,1,0:T(8,128)(2,1)}), bf16[4,8,64,896]{3,2,1,0:T(8,128)(2,1)}, u32[]{:S(2)}, u32[]{:S(2)}) %all-to-all-start) | async-done | bytes 3670048 | tf_op jit(solution)/shard_map/all_to_all | solution.py:19
  54.0 4.9 %copy.11 = bf16[8,64,4,896]{3,2,1,0:T(4,128)(2,1)S(1)} copy(bf16[8,64,4,896]{3,1,0,2:T(8,128)(2,1)} %bitcast) | data formatting | bytes 7340032 | tf_op jit(solution)/shard_map/transpose | solution.py:12
  58.9 2.4 %copy.12 = bf16[64,8,4,896]{3,1,2,0:T(8,128)(2,1)} copy(bf16[64,8,4,896]{3,2,1,0:T(4,128)(2,1)S(1)} %bitcast.11) | data formatting | bytes 7340032
  61.3 0.0 copy-start.4
  61.3 0.0 copy-start.5
  61.3 43.5 %all-gather.3.cloned.1.call-done = bf16[128,28,1024]{2,1,0:T(8,128)(2,1)} async-done(((bf16[1,28,1024]{2,1,0:T(8,128)(2,1)}), bf16[128,28,1024]{2,1,0:T(8,128)(2,1)}) %all-gather.3.cloned.1.call-update) | async-done | bytes 7340048 | tf_op jit(solution)/shard_map/all_gather | solution.py:34
  104.8 10.9 %reshape.16 = bf16[3584,1024]{1,0:T(8,128)(2,1)} reshape(bf16[128,28,1024]{2,1,0:T(8,128)(2,1)} %all-gather.3.cloned.1.call-done) | data formatting | bytes 14680064
  115.7 0.0 copy-done.4
  115.7 0.0 copy-done.5
  115.7 0.0 copy-start
  115.7 0.0 copy-start.1
  115.8 8.3 %multiply_reduce_fusion = f32[512]{0:T(512)S(1)} fusion(bf16[512,3584]{1,0:T(8,128)(2,1)} %bitcast.12, bf16[3584,1024]{1,0:T(8,128)(2,1)} %reshape.16, f32[1024]{0:T(1024)S(1)} %copy-done.4, f32[1024]{0:T(1024)S(1)} %copy-done.5), kind=kOutput, calls=%fused_computation | convolution fusion | flops 3760193024 | bytes 11020288 | tf_op jit(solution)/shard_map/dot_general | solution.py:33
  124.0 0.1 broadcast_in_dim.48
  124.1 0.0 copy-done
  124.1 0.3 select_reduce_fusion
  124.4 12.0 %psum.28 = f32[8,64]{1,0:T(8,128)S(1)} all-reduce(f32[8,64]{1,0:T(8,128)S(1)} %select_reduce_fusion), channel_id=1, replica_groups=mesh['seq_0'=8,'seq_1'=8,'seq_2'=2,'head'=4] {'seq_0'}, use_global_device_ids=true, to_apply=%region_2.3 | all-reduce | flops 512 | bytes 4096 | tf_op jit(solution)/shard_map/psum | solution.py:28
  136.4 12.1 %psum.29 = f32[8,64]{1,0:T(8,128)S(1)} all-reduce(f32[8,64]{1,0:T(8,128)S(1)} %psum.28), channel_id=1, replica_groups=mesh['seq_0'=8,'seq_1'=8,'seq_2'=2,'head'=4] {'seq_1'}, use_global_device_ids=true, to_apply=%region_3.4 | all-reduce | flops 512 | bytes 4096 | tf_op jit(solution)/shard_map/psum | solution.py:28
  148.5 9.8 %psum.30 = f32[8,64]{1,0:T(8,128)S(1)} all-reduce(f32[8,64]{1,0:T(8,128)S(1)} %psum.29), channel_id=1, replica_groups=mesh['seq_0'=8,'seq_1'=8,'seq_2'=2,'head'=4] {'seq_2'}, use_global_device_ids=true, to_apply=%region_4.5 | all-reduce | flops 512 | bytes 4096 | tf_op jit(solution)/shard_map/psum | solution.py:28
  158.3 8.4 %psum.31 = f32[8,64]{1,0:T(8,128)S(1)} all-reduce(f32[8,64]{1,0:T(8,128)S(1)} %psum.30), channel_id=1, replica_groups=mesh['seq_0'=8,'seq_1'=8,'seq_2'=2,'head'=4] {'head'}, use_global_device_ids=true, to_apply=%region_5.6 | all-reduce | flops 512 | bytes 4096 | tf_op jit(solution)/shard_map/psum | solution.py:28
  166.7 0.0 copy-done.1
  166.7 0.1 select_reduce_fusion.3
  166.8 0.0 copy-start.2
  166.8 0.6 broadcast_select_fusion
  167.4 0.2 select_reduce_fusion.1
  167.6 0.5 sub.3
  168.2 0.0 copy-done.2
  (2 shorter events, 0.0 us)
Async XLA Ops:
  7.2 97.6 %all-gather.3.cloned.1.call-start = ((), (), s32[]{:S(2)}) async-start(), calls=%async_computation.1 | async-start | bytes 8454144 | tf_op jit(solution)/shard_map/all_gather | solution.py:34
  11.5 5.0 %copy-start.3 = (s32[8,2]{0,1:T(2,128)S(1)}, s32[8,2]{0,1:T(2,128)}, u32[]{:S(2)}) copy-start(s32[8,2]{0,1:T(2,128)} %param.10) | copy-start | bytes 196
  11.5 42.6 %all-to-all-start = ((bf16[4,8,64,896]{3,2,1,0:T(8,128)(2,1)}), bf16[4,8,64,896]{3,2,1,0:T(8,128)(2,1)}, u32[]{:S(2)}, u32[]{:S(2)}) async-start(bf16[4,8,64,896]{3,2,1,0:T(8,128)(2,1)} %broadcast_in_dim.47), calls=%async_computation | async-start | bytes 7340032 | tf_op jit(solution)/shard_map/all_to_all | solution.py:19
  61.3 54.4 %copy-start.4 = (f32[1024]{0:T(1024)S(1)}, f32[1024]{0:T(1024)}, u32[]{:S(2)}) copy-start(f32[1024]{0:T(1024)} %param.13) | copy-start | bytes 12292
  61.3 54.4 %copy-start.5 = (f32[1024]{0:T(1024)S(1)}, f32[1024]{0:T(1024)}, u32[]{:S(2)}) copy-start(f32[1024]{0:T(1024)} %param.12) | copy-start | bytes 12292
  115.7 8.4 %copy-start = (s32[8,64]{1,0:T(8,128)S(1)}, s32[8,64]{1,0:T(8,128)}, u32[]{:S(2)}) copy-start(s32[8,64]{1,0:T(8,128)} %param.8) | copy-start | bytes 6148
  115.7 51.0 %copy-start.1 = (s32[8,64]{1,0:T(8,128)S(1)}, s32[8,64]{1,0:T(8,128)}, u32[]{:S(2)}) copy-start(s32[8,64]{1,0:T(8,128)} %param.9) | copy-start | bytes 6148
  166.8 1.3 copy-start.2
Sparse Core Ops, SparseCore 0:
  11.1 93.6 all-gather.2
where the time goes:
time: 176 us; the launch traced here: 175 us
  waiting for transfers between devices  81.7 us (46%)
  blocking collectives  42.3 us (24%)
  local copies, waits for them, and re-layouts  21.9 us (12%)
  between operations  14.1 us (8%)
  matrix products  8.25 us (5%)
  starting transfers between devices  5 us (3%)
    all_gather x1, waiting for transfers between devices, score_rows(): lax.all_gather(w_first, SEQ, axis=0, tiled=True)  43.5 us
    psum x4, blocking collectives, over_axes(): shard = lax.psum(shard, axis)  42.3 us
    all_to_all x1, waiting for transfers between devices, sent_to_all(): return lax.all_to_all(copies, axis, split_axis=0, concat_axis=0, tiled=True)  37.6 us
    unnamed x14, local copies, waits for them, and re-layouts  13.4 us
    dot_general x1, matrix products, score_rows(): jnp.dot(rows, lax.all_gather(w_first, SEQ, axis=0, tiled=True), preferred...  8.25 us
    all_to_all x1, starting transfers between devices, sent_to_all(): return lax.all_to_all(copies, axis, split_axis=0, concat_axis=0, tiled=True)  4.96 us
    transpose x1, local copies, waits for them, and re-layouts, laid_out(): pieces = jnp.moveaxis(pieces, 0, dim)  4.88 us
    broadcast_in_dim x1, local copies, waits for them, and re-layouts, sent_to_all(): copies = jnp.broadcast_to(shard, (lax.axis_size(axis), *shard.shape))  3.55 us
  transfers between devices with their start and end apart: 2, of which 2 were waited for; matrix products, arithmetic and copies ran while one was open for 6% of the time, Pallas kernels for 0%

commit v1 on v0

v1 whole, which is shorter than its diff:
```python
import jax
import jax.numpy as jnp
from jax import lax
from jax.experimental import pallas as pl
from jax.experimental.pallas import tpu as pltpu
from jax.sharding import Mesh
from jax.sharding import PartitionSpec as P

NY, NZ, NC, NX = 8, 8, 2, 4
ZC = NZ * NC
SEQ = ("y", "z", "c")
XZC = ("x", "z", "c")
ALL = ("y", "z", "c", "x")
SLOTS = 16
ROUND_SLOTS = 6
CAP = 96
HALF = CAP // 2
VMEM = pl.BlockSpec(memory_space=pltpu.VMEM)
SMEM = pl.BlockSpec(memory_space=pltpu.SMEM)
F32, BF16, I32 = jnp.float32, jnp.bfloat16, jnp.int32
HIGH = lax.Precision.HIGHEST


def iota(shape, dim):
    return lax.broadcasted_iota(I32, shape, dim)


def pick_kernel(scalars, boundary_ref, hidden_ref, out_ref):
    me, low = scalars[0], scalars[1]
    traces, steps = boundary_ref.shape
    tokens = hidden_ref.shape[1]
    bound = boundary_ref[...]
    local = bound - me * tokens
    mine = (local >= 0) & (local < tokens)
    owned = jnp.where(mine, 1.0, 0.0).astype(BF16)
    before = jnp.where(iota((steps, steps), 0) < iota((steps, steps), 1), 1.0, 0.0).astype(BF16)
    within = jnp.dot(owned, before, preferred_element_type=F32)
    totals = jnp.dot(owned, jnp.ones((steps, steps), BF16), preferred_element_type=F32)
    earlier = jnp.where(iota((traces, traces), 1) < iota((traces, traces), 0), 1.0, 0.0)
    carried = jnp.dot(earlier.astype(BF16), totals.astype(BF16), preferred_element_type=F32)
    slot = jnp.where(mine, (within + carried).astype(I32) - low, -1)
    picked = jnp.zeros((SLOTS, hidden_ref.shape[2]), F32)
    for t in range(traces):
        hit = slot[t : t + 1, :] == iota((SLOTS, steps), 0)
        token = jnp.sum(jnp.where(hit, local[t : t + 1, :] + 1, 0).astype(F32), axis=1, keepdims=True)
        choose = jnp.where(token.astype(I32) == iota((SLOTS, tokens), 1) + 1, 1.0, 0.0).astype(BF16)
        picked += jnp.dot(choose, hidden_ref[t], preferred_element_type=F32)
    depth = hidden_ref.shape[2] // 2 // ZC
    half = hidden_ref.shape[2] // 2
    pad = jnp.zeros((SLOTS, 32 - depth), F32)
    for zc in range(ZC):
        parts = []
        for b in range(2):
            start = b * half + zc * depth
            parts += [picked[:, start : start + depth], pad]
        piece = jnp.concatenate(parts, axis=1)
        piece = jnp.concatenate([piece[: SLOTS // 2], piece[SLOTS // 2 :]], axis=1).astype(BF16)
        for x in range(NX):
            out_ref[x * ZC + zc] = piece


def layer_kernel(scalars, boundary_ref, picks_ref, weight_ref, out_ref):
    me, low, window = scalars[0], scalars[1], scalars[2]
    owner = boundary_ref[...] >> 6
    plane = me // ZC
    lane = iota((1, 128), 1)
    count = jnp.zeros((1, 128), F32)
    start = jnp.zeros((1, 128), F32)
    top = window.astype(F32)
    for zc in range(ZC):
        here = jnp.where(owner == plane * ZC + zc, 1.0, 0.0)
        number = jnp.sum(jnp.sum(here, axis=0, keepdims=True), axis=1, keepdims=True)
        number = jnp.clip(number - low.astype(F32), 0.0, top)
        count = count + jnp.where(lane // 8 == zc, number, 0.0)
        start = start + jnp.where(lane // 8 > zc, number, 0.0)
    count, start = count.astype(I32), start.astype(I32)
    choices = []
    for h in range(2):
        slot = lane % 8 + h * 8
        place = jnp.where(slot < count, start + slot, -1)
        choices.append(jnp.where(place == iota((CAP, 128), 0), 1.0, 0.0).astype(BF16))
    parts = []
    for x in range(NX):
        block = picks_ref[x * ZC : (x + 1) * ZC].reshape(ZC * 8, 128)
        left = jnp.dot(choices[0], block, preferred_element_type=F32)
        right = jnp.dot(choices[1], block, preferred_element_type=F32)
        parts.append(left[:, :64] + right[:, 64:])
    rows = jnp.concatenate(parts, axis=1).astype(BF16)
    weight = weight_ref[...].reshape(NY * 32, weight_ref.shape[2])
    partial = jnp.dot(rows, weight, preferred_element_type=F32)
    for h in range(2):
        for j in range(8):
            out_ref[h * 8 + j] = partial[h * HALF : (h + 1) * HALF, j * 128 : (j + 1) * 128]


def head_kernel(scalars, pre_ref, bias_ref, second_ref, out_ref):
    j = scalars[0] % 8
    pre = pre_ref[0]
    for zc in range(1, ZC):
        pre = pre + pre_ref[zc]
    unit = jnp.maximum(pre + bias_ref[pl.ds(j, 1), :], 0.0) * second_ref[pl.ds(j, 1), :]
    unit = jnp.concatenate([unit, jnp.zeros((128 - HALF, 128), F32)], axis=0)
    logit = lax.dot_general(
        jnp.ones((8, 128), F32), unit, (((1,), (1,)), ((), ())), precision=HIGH, preferred_element_type=F32
    )
    out_ref[...] = jnp.broadcast_to(logit[0:1, :].reshape(1, 1, 128), out_ref.shape)


def look_up_kernel(logit_ref, place_ref, out_ref):
    rows = []
    for y in range(NY):
        for h in range(2):
            first = y * ZC * NX + h * 8 * NX
            rows.append(jnp.sum(logit_ref[first : first + 8 * NX].reshape(8 * NX, 128), axis=0, keepdims=True))
    table = jnp.concatenate(rows, axis=0)
    place = place_ref[...]
    for t in range(place.shape[0]):
        row, lane = place[t : t + 1, :] // 128, place[t : t + 1, :] % 128
        spread = jnp.where(iota((128, place.shape[1]), 0) == lane, 1.0, 0.0)
        found = jnp.dot(table, spread, precision=HIGH, preferred_element_type=F32)
        found = jnp.where(iota(found.shape, 0) == row, found, 0.0)
        out_ref[t : t + 1, :] = jnp.sum(found, axis=0, keepdims=True)


def finish_kernel(logit_ref, valid_ref, pairs_ref, reward_ref, score_ref, margin_ref):
    logit = logit_ref[...]
    live = valid_ref[...] == 1
    reward_ref[...] = jnp.where(live, logit, 0.0)
    score = jnp.min(jnp.where(live, logit, 1e30), axis=1, keepdims=True)
    traces = logit.shape[0]
    diagonal = iota((traces, traces), 0) == iota((traces, traces), 1)
    flat = jnp.sum(jnp.where(diagonal, score, 0.0), axis=0, keepdims=True)
    score_ref[...] = flat
    trace = iota((traces, traces), 1)
    pairs = pairs_ref[...]
    ends = []
    for e in range(2):
        end = jnp.sum(jnp.where(pairs[:, e : e + 1] == trace, flat, 0.0), axis=1, keepdims=True)
        ends.append(end)
    margin_ref[...] = jnp.sum(jnp.where(diagonal, ends[0] - ends[1], 0.0), axis=0, keepdims=True)


def call(kernel, specs, shape, *args):
    single = not isinstance(shape, list)
    return pl.pallas_call(
        kernel,
        out_shape=shape,
        in_specs=specs,
        out_specs=VMEM if single else [VMEM] * len(shape),
        name=kernel.__name__,
    )(*args)


def exchange(pieces, axes):
    return lax.all_to_all(pieces, axes, split_axis=0, concat_axis=0, tiled=True)


def per_device(hidden_states, boundary, valid, pairs, w_first, b_first, w_second):
    columns = w_first.shape[1]
    me = lax.axis_index(SEQ).astype(I32)
    weight = jnp.pad(w_first, ((0, 32 - w_first.shape[0]), (0, 0)))
    weight = exchange(jnp.broadcast_to(weight, (NY, *weight.shape)), "y")
    bias, second = b_first.reshape(8, columns // 8), w_second.reshape(8, columns // 8)

    owner = (boundary >> 6).reshape(-1)
    order = jnp.arange(owner.shape[0], dtype=I32)
    same = owner[:, None] == owner[None, :]
    rank = jnp.sum(same & (order[None, :] < order[:, None]), axis=1, dtype=I32)
    most = jnp.max(rank) + 1
    plane = owner // ZC
    crowd = jnp.max(jnp.sum(plane[:, None] == plane[None, :], axis=1, dtype=I32))
    window = jnp.where((most <= SLOTS) & (crowd <= CAP), SLOTS, ROUND_SLOTS).astype(I32)

    def one_round(low, window):
        scalars = jnp.stack([me, low, window])
        picks = call(
            pick_kernel, [SMEM, VMEM, VMEM], jax.ShapeDtypeStruct((NX * ZC, 8, 128), BF16),
            scalars, boundary, hidden_states,
        )
        picks = exchange(picks, XZC)
        pre = call(
            layer_kernel, [SMEM, VMEM, VMEM, VMEM], jax.ShapeDtypeStruct((ZC, HALF, 128), F32),
            scalars, boundary, picks, weight,
        )
        pre = exchange(pre, ("z", "c"))
        share = call(
            head_kernel, [SMEM, VMEM, VMEM, VMEM], jax.ShapeDtypeStruct((NY * ZC * NX, 1, 128), F32),
            scalars, pre, bias, second,
        )
        share = exchange(share, ALL)
        inside = (rank >= low) & (rank < low + window)
        ahead = inside[None, :] & (plane[None, :] == plane[:, None]) & (owner[None, :] < owner[:, None])
        g = jnp.sum(ahead, axis=1, dtype=I32) + rank - low
        place = (plane * 2 + g // HALF) * 128 + g % HALF
        place = jnp.where(inside, place, -128).reshape(boundary.shape)
        return call(look_up_kernel, [VMEM, VMEM], jax.ShapeDtypeStruct(boundary.shape, F32), share, place)

    logit = one_round(jnp.int32(0), window)

    def more(state):
        low, total = state
        return low + ROUND_SLOTS, total + one_round(low, jnp.int32(ROUND_SLOTS))

    _, logit = lax.while_loop(lambda state: state[0] < most, more, (window, logit))
    reward, score, margin = call(
        finish_kernel, [VMEM] * 3,
        [jax.ShapeDtypeStruct(boundary.shape, F32)] + [jax.ShapeDtypeStruct((1, 8), F32)] * 2,
        logit, valid, pairs,
    )
    return reward, score.reshape(8), margin.reshape(8)


def solution(mesh):
    torus = Mesh(mesh.devices.reshape(NY, NZ, NC, NX), ALL)
    return jax.shard_map(
        per_device,
        mesh=torus,
        in_specs=(P(None, SEQ, "x"), P(), P(), P(), P(SEQ, "x"), P("x"), P("x")),
        out_specs=(P(), P(), P()),
        check_vma=False,
    )
```

time: 176 us -> 110 us (0.62)
  waiting for transfers between devices: 81.7 us -> 37.5 us
  starting transfers between devices: 5 us -> 28.6 us
  blocking collectives: 42.3 us -> 23.3 us
  local copies, waits for them, and re-layouts: 21.9 us -> 3.92 us
  between operations: 14.1 us -> 2.05 us
  Pallas kernels: 0 us -> 9.9 us
  matrix products: 8.25 us -> 0 us
  other arithmetic: 1.71 us -> 4.16 us
    all_gather x1 -> x0, waiting for transfers between devices: 43.5 us -> none  [score_rows(): lax.all_gather(w_first, SEQ, axis=0, tiled=True)]
    psum x4 -> x0, blocking collectives: 42.3 us -> none  [over_axes(): shard = lax.psum(shard, axis)]
    all_to_all x1 -> x3, starting transfers between devices: 4.96 us -> 28.6 us  [exchange(): return lax.all_to_all(pieces, axes, split_axis=0, concat_axis=0, tiled=True)]
    all_to_all x0 -> x1, blocking collectives: none -> 23.3 us  [exchange(): return lax.all_to_all(pieces, axes, split_axis=0, concat_axis=0, tiled=True)]
    unnamed x14 -> x21, local copies, waits for them, and re-layouts: 13.4 us -> 3.39 us
    pallas_call x0 -> x5, Pallas kernels: none -> 9.9 us  [call(): pl.pallas_call(kernel, out_shape=shape, in_specs=specs, out_specs=VMEM if...]
    dot_general x1 -> x0, matrix products: 8.25 us -> none  [score_rows(): jnp.dot(rows, lax.all_gather(w_first, SEQ, axis=0, tiled=True), preferred...]
    transpose x1 -> x0, local copies, waits for them, and re-layouts: 4.88 us -> none  [laid_out(): pieces = jnp.moveaxis(pieces, 0, dim)]
  transfers between devices with their start and end apart: 2 -> 3, of which waited for: 2 -> 3; matrix products, arithmetic and copies ran while one was open for 6% -> 2% of each run, Pallas kernels for 0% -> 0%
where the time goes in v1:
time: 110 us
  waiting for transfers between devices  37.5 us (34%)
  starting transfers between devices  28.6 us (26%)
  blocking collectives  23.3 us (21%)
  Pallas kernels  9.9 us (9%)
  other arithmetic  4.16 us (4%)
  local copies, waits for them, and re-layouts  3.92 us (4%)
  between operations  2.05 us (2%)
    all_to_all x3, waiting for transfers between devices, exchange(): return lax.all_to_all(pieces, axes, split_axis=0, concat_axis=0, tiled=True)  37.5 us
    all_to_all x3, starting transfers between devices, exchange(): return lax.all_to_all(pieces, axes, split_axis=0, concat_axis=0, tiled=True)  28.6 us
    all_to_all x1, blocking collectives, exchange(): return lax.all_to_all(pieces, axes, split_axis=0, concat_axis=0, tiled=True)  23.3 us
    pallas_call x5, Pallas kernels, call(): pl.pallas_call(kernel, out_shape=shape, in_specs=specs, out_specs=VMEM if...  9.9 us
    unnamed x21, local copies, waits for them, and re-layouts  3.39 us
  transfers between devices with their start and end apart: 3, of which 3 were waited for; matrix products, arithmetic and copies ran while one was open for 2% of the time, Pallas kernels for 0%

profile of v1, /device:TPU:1, one launch (start us, length us, event | category | flops | bytes accessed | tf_op | source)
XLA Modules:
  0.0 109.6 jit_solution(8419689018986148931)
XLA Ops:
  0.6 0.7 broadcast_shift-right-arithmetic_fusion
  1.3 0.0 copy-start.10
  1.3 0.1 eq.65
  1.4 0.3 convert_reduce_fusion.3
  1.7 0.2 convert_reduce_fusion.2
  1.9 0.6 reduce_max.18
  2.6 0.6 reduce_max.19
  4.5 0.0 copy-start.5
  4.5 0.6 pad_add_fusion.1.scalars
  5.1 0.1 copy-done.5
  5.2 2.6 %pick_kernel.5 = bf16[64,8,128]{2,1,0:T(8,128)(2,1)} custom-call(s32[3]{0:T(128)} %pad_add_fusion.1.scalars, s32[8,64]{1,0:T(8,128)S(1)} %copy-done.5, bf16[8,64,896]{2,1,0:T(8,128)(2,1)} %hidden_ref.1), custom_call_target="tpu_custom_call" | custom-call | tf_op jit(solution)/shard_map/pick_kernel/pallas_call | solution.py:145
  7.8 0.0 copy-start.9
  7.8 15.0 %all-to-all-start.3 = ((bf16[64,8,128]{2,1,0:T(8,128)(2,1)}), bf16[64,8,128]{2,1,0:T(8,128)(2,1)S(1)}, u32[]{:S(2)}, u32[]{:S(2)}) async-start(bf16[64,8,128]{2,1,0:T(8,128)(2,1)} %pick_kernel.5), calls=%async_computation.3 | async-start | bytes 262144 | tf_op jit(solution)/shard_map/all_to_all | solution.py:155
  22.7 0.0 copy-done.9
  22.8 10.3 %all-to-all-done.3.picks_ref = bf16[64,8,128]{2,1,0:T(8,128)(2,1)S(1)} async-done(((bf16[64,8,128]{2,1,0:T(8,128)(2,1)}), bf16[64,8,128]{2,1,0:T(8,128)(2,1)S(1)}, u32[]{:S(2)}, u32[]{:S(2)}) %all-to-all-start.3) | async-done | bytes 131104 | tf_op jit(solution)/shard_map/all_to_all | solution.py:155
  33.1 0.0 copy-start.6
  33.1 0.6 copy-done.6
  33.7 23.3 %all_to_all.41.weight_ref = bf16[8,32,1024]{2,1,0:T(8,128)(2,1)S(1)} all-to-all(bf16[8,32,1024]{2,1,0:T(8,128)(2,1)S(1)} %broadcast_in_dim.8), channel_id=1, replica_groups=mesh['y'=8,'z'=8,'c'=2,'x'=4] {'y'}, dimensions={0} | all-to-all | bytes 1048576 | tf_op jit(solution)/shard_map/all_to_all | solution.py:155
  57.0 2.3 %layer_kernel.5 = f32[16,48,128]{2,1,0:T(8,128)} custom-call(s32[3]{0:T(128)} %pad_add_fusion.1.scalars, s32[8,64]{1,0:T(8,128)S(1)} %copy-done.5, bf16[64,8,128]{2,1,0:T(8,128)(2,1)} %copy-done.6, bf16[8,32,1024]{2,1,0:T(8,128)(2,1)S(1)} %all_to_all.41.weight_ref), custom_call_target="tpu_custom_call" | custom-call | tf_op jit(solution)/shard_map/layer_kernel/pallas_call | solution.py:145
  59.3 0.0 copy-start.7
  59.3 0.0 copy-start.8
  59.3 5.3 %all-to-all-start.5 = ((f32[16,48,128]{2,1,0:T(8,128)}), f32[16,48,128]{2,1,0:T(8,128)S(1)}, u32[]{:S(2)}, u32[]{:S(2)}) async-start(f32[16,48,128]{2,1,0:T(8,128)} %layer_kernel.5), calls=%async_computation.5 | async-start | bytes 786432 | tf_op jit(solution)/shard_map/all_to_all | solution.py:155
  64.6 0.0 copy-start.1
  64.6 0.5 convert_reduce_fusion.1
  65.0 14.0 %all-to-all-done.5.pre_ref = f32[16,48,128]{2,1,0:T(8,128)S(1)} async-done(((f32[16,48,128]{2,1,0:T(8,128)}), f32[16,48,128]{2,1,0:T(8,128)S(1)}, u32[]{:S(2)}, u32[]{:S(2)}) %all-to-all-start.5) | async-done | bytes 393248 | tf_op jit(solution)/shard_map/all_to_all | solution.py:155
  79.1 0.0 copy-start.3
  79.1 0.7 copy-done.3
  79.8 0.0 copy-done.7
  79.8 0.0 copy-done.8
  79.8 2.0 %head_kernel.5 = f32[512,1,128]{2,1,0:T(1,128)} custom-call(s32[3]{0:T(128)} %pad_add_fusion.1.scalars, f32[16,48,128]{2,1,0:T(8,128)} %copy-done.3, f32[8,128]{1,0:T(8,128)S(1)} %bitcast.14, f32[8,128]{1,0:T(8,128)S(1)} %bitcast.16), custom_call_target="tpu_custom_call" | custom-call | tf_op jit(solution)/shard_map/head_kernel/pallas_call | solution.py:145
  81.8 8.4 %all-to-all-start.6 = ((f32[512,1,128]{2,1,0:T(1,128)}), f32[512,1,128]{2,1,0:T(1,128)S(1)}, u32[]{:S(2)}, u32[]{:S(2)}) async-start(f32[512,1,128]{2,1,0:T(1,128)} %head_kernel.5), calls=%async_computation.6 | async-start | bytes 524288 | tf_op jit(solution)/shard_map/all_to_all | solution.py:155
  90.2 0.1 and.123
  90.3 0.0 copy-done.10
  90.3 0.1 lt.129
  90.4 0.1 div.50
  90.5 0.1 rem.90
  90.5 0.0 copy-start.11
  90.5 0.1 ne.110
  90.6 0.6 copy-done.11
  91.2 0.7 copy.11.pairs_ref
  91.9 0.6 fusion.10.place_ref
  92.5 13.2 %all-to-all-done.6.logit_ref = f32[512,1,128]{2,1,0:T(1,128)S(1)} async-done(((f32[512,1,128]{2,1,0:T(1,128)}), f32[512,1,128]{2,1,0:T(1,128)S(1)}, u32[]{:S(2)}, u32[]{:S(2)}) %all-to-all-start.6) | async-done | bytes 262176 | tf_op jit(solution)/shard_map/all_to_all | solution.py:155
  105.7 0.0 copy-start.4
  105.7 0.7 copy-done.4
  106.4 1.6 %look_up_kernel.5 = f32[8,64]{1,0:T(8,128)S(1)} custom-call(f32[512,1,128]{2,1,0:T(1,128)} %copy-done.4, s32[8,64]{1,0:T(8,128)} %fusion.10.place_ref), custom_call_target="tpu_custom_call" | custom-call | tf_op jit(solution)/shard_map/look_up_kernel/pallas_call | solution.py:145
  108.0 0.0 copy-done.1
  108.0 0.2 while.13
  108.2 1.4 %finish_kernel.1 = (f32[8,64]{1,0:T(8,128)}, f32[1,8]{1,0:T(1,128)}, f32[1,8]{1,0:T(1,128)}) custom-call(f32[8,64]{1,0:T(8,128)S(1)} %get-tuple-element.156.logit_ref, s32[8,64]{1,0:T(8,128)} %valid_ref.1, s32[8,2]{1,0:T(8,128)} %copy.11.pairs_ref), custom_call_target="tpu_custom_call" | custom-call | tf_op jit(solution)/shard_map/finish_kernel/pallas_call | solution.py:145
  (6 shorter events, 0.1 us)
Async XLA Ops:
  1.3 89.0 %copy-start.10 = (s32[8,64]{1,0:T(8,128)}, s32[8,64]{1,0:T(8,128)S(1)}, u32[]{:S(2)}) copy-start(s32[8,64]{1,0:T(8,128)S(1)} %broadcast_shift-right-arithmetic_fusion) | copy-start | bytes 6148
  4.5 0.7 copy-start.5
  7.8 15.0 %copy-start.9 = (bf16[28,1024]{1,0:T(8,128)(2,1)S(1)}, bf16[28,1024]{1,0:T(8,128)(2,1)}, u32[]{:S(2)}) copy-start(bf16[28,1024]{1,0:T(8,128)(2,1)} %param.13) | copy-start | bytes 172036
  7.8 25.3 %all-to-all-start.3 = ((bf16[64,8,128]{2,1,0:T(8,128)(2,1)}), bf16[64,8,128]{2,1,0:T(8,128)(2,1)S(1)}, u32[]{:S(2)}, u32[]{:S(2)}) async-start(bf16[64,8,128]{2,1,0:T(8,128)(2,1)} %pick_kernel.5), calls=%async_computation.3 | async-start | bytes 262144 | tf_op jit(solution)/shard_map/all_to_all | solution.py:155
  33.1 0.7 copy-start.6
  59.3 20.5 %copy-start.7 = (f32[1024]{0:T(1024)S(1)}, f32[1024]{0:T(1024)}, u32[]{:S(2)}) copy-start(f32[1024]{0:T(1024)} %param.14) | copy-start | bytes 12292
  59.3 20.5 %copy-start.8 = (f32[1024]{0:T(1024)S(1)}, f32[1024]{0:T(1024)}, u32[]{:S(2)}) copy-start(f32[1024]{0:T(1024)} %param.15) | copy-start | bytes 12292
  59.3 19.8 %all-to-all-start.5 = ((f32[16,48,128]{2,1,0:T(8,128)}), f32[16,48,128]{2,1,0:T(8,128)S(1)}, u32[]{:S(2)}, u32[]{:S(2)}) async-start(f32[16,48,128]{2,1,0:T(8,128)} %layer_kernel.5), calls=%async_computation.5 | async-start | bytes 786432 | tf_op jit(solution)/shard_map/all_to_all | solution.py:155
  64.6 43.4 %copy-start.1 = (bf16[8,64,896]{2,1,0:T(8,128)(2,1)S(1)}, bf16[8,64,896]{2,1,0:T(8,128)(2,1)}, u32[]{:S(2)}) copy-start(bf16[8,64,896]{2,1,0:T(8,128)(2,1)} %hidden_ref.1) | copy-start | bytes 2752516
  79.1 0.7 copy-start.3
  81.8 23.8 %all-to-all-start.6 = ((f32[512,1,128]{2,1,0:T(1,128)}), f32[512,1,128]{2,1,0:T(1,128)S(1)}, u32[]{:S(2)}, u32[]{:S(2)}) async-start(f32[512,1,128]{2,1,0:T(1,128)} %head_kernel.5), calls=%async_computation.6 | async-start | bytes 524288 | tf_op jit(solution)/shard_map/all_to_all | solution.py:155
  90.5 0.7 copy-start.11
  105.7 0.7 copy-start.4

commit v2 on v0

v2 whole, which is shorter than its diff:
```python
import jax
import jax.numpy as jnp
from jax import lax
from jax.experimental import pallas as pl
from jax.experimental.pallas import tpu as pltpu
from jax.sharding import Mesh
from jax.sharding import PartitionSpec as P

NYH, NY0, NZH, NZ0, NC, NX = 4, 2, 4, 2, 2, 4
NAMES = ("yh", "y0", "zh", "z0", "c", "x")
SEQ = NAMES[:5]
OWNERS = NYH * NY0 * NZ0 * NC
BLOCKS = NY0 * NZ0 * NC
SLOTS = 16
ROUND_SLOTS = 3
PART = 30
CAP = NX * PART
DEEP = 32
VMEM = pl.BlockSpec(memory_space=pltpu.VMEM)
SMEM = pl.BlockSpec(memory_space=pltpu.SMEM)
F32, BF16, I32 = jnp.float32, jnp.bfloat16, jnp.int32
HIGH = lax.Precision.HIGHEST


def iota(shape, dim):
    return lax.broadcasted_iota(I32, shape, dim)


def ones_where(test, dtype=F32):
    return jnp.where(test, 1.0, 0.0).astype(dtype)


def group_of(owner):
    return (owner >> 2) & 3


def pick_kernel(round_ref, boundary_ref, valid_ref, hidden_ref, out_ref):
    me, low = lax.axis_index(SEQ), round_ref[0]
    traces, steps = boundary_ref.shape
    tokens = hidden_ref.shape[1]
    local = boundary_ref[...] - me * tokens
    mine = (local >= 0) & (local < tokens) & (valid_ref[...] == 1)
    owned = ones_where(mine, BF16)
    before = ones_where(iota((steps, steps), 0) < iota((steps, steps), 1), BF16)
    within = jnp.dot(owned, before, preferred_element_type=F32)
    totals = jnp.dot(owned, jnp.ones((steps, steps), BF16), preferred_element_type=F32)
    earlier = ones_where(iota((traces, traces), 1) < iota((traces, traces), 0), BF16)
    carried = jnp.dot(earlier, totals.astype(BF16), preferred_element_type=F32)
    slot = jnp.where(mine, (within + carried).astype(I32) - low, -1)
    picked = jnp.zeros((SLOTS, hidden_ref.shape[2]), F32)
    for t in range(traces):
        hit = slot[t : t + 1, :] == iota((SLOTS, steps), 0)
        token = jnp.sum(jnp.where(hit, local[t : t + 1, :] + 1, 0).astype(F32), axis=1, keepdims=True)
        choose = ones_where(token.astype(I32) == iota((SLOTS, tokens), 1) + 1, BF16)
        picked += jnp.dot(choose, hidden_ref[t], preferred_element_type=F32)
    depth = hidden_ref.shape[2] // (BLOCKS * NZH)
    pad = jnp.zeros((SLOTS, DEEP - depth), F32)
    for y0 in range(NY0):
        for low2 in range(NZ0 * NC):
            parts = []
            for zh in range(NZH):
                start = (y0 * 16 + zh * 4 + low2) * depth
                parts += [picked[:, start : start + depth], pad]
            piece = jnp.concatenate(parts, axis=1).astype(BF16)
            for yh in range(NYH):
                out_ref[yh * BLOCKS + y0 * 4 + low2] = piece


def layer_kernel(round_ref, boundary_ref, valid_ref, picks_ref, weight_ref, bias_ref, second_ref, out_ref):
    low, window = round_ref[0], round_ref[1]
    traces, steps = boundary_ref.shape
    owner = jnp.where(valid_ref[...] == 1, boundary_ref[...] >> 6, -1)
    count = jnp.zeros((128, steps), F32)
    for t in range(traces):
        count += ones_where(owner[t : t + 1, :] == iota((128, steps), 0))
    count = jnp.sum(count, axis=1, keepdims=True)
    device = iota((128, 1), 0)
    most = jnp.max(count, axis=0, keepdims=True)
    fits = most <= SLOTS
    for zh in range(NZH):
        crowd = jnp.sum(jnp.where(group_of(device) == zh, count, 0.0), axis=0, keepdims=True)
        fits = fits & (crowd <= CAP)
    top = jnp.where(window > 0, window.astype(F32), jnp.where(fits, float(SLOTS), float(ROUND_SLOTS)))
    count = jnp.clip(count - low.astype(F32), 0.0, top)
    mine = group_of(device) == lax.axis_index("zh")
    count = jnp.where(mine, count, 0.0)
    place_in_group = (device >> 4) * 4 + (device & 3)
    lane = iota((128, OWNERS * SLOTS), 1) >> 4
    number = jnp.sum(jnp.where(lane == place_in_group, count, 0.0), axis=0, keepdims=True).astype(I32)
    start = jnp.sum(jnp.where(lane > place_in_group, count, 0.0), axis=0, keepdims=True).astype(I32)
    slot = iota((1, OWNERS * SLOTS), 1) & (SLOTS - 1)
    g = start + slot
    g = g + 2 * ((g >= PART).astype(I32) + (g >= 2 * PART).astype(I32) + (g >= 3 * PART).astype(I32))
    g = jnp.where(slot < number, g, -1)
    choose = ones_where(g == iota((NX * DEEP, OWNERS * SLOTS), 0), BF16)
    rows = jnp.dot(choose, picks_ref[...].reshape(OWNERS * SLOTS, 128), preferred_element_type=F32)
    weight = weight_ref[...].reshape(NZH * DEEP, weight_ref.shape[2])
    partial = jnp.dot(rows.astype(BF16), weight, preferred_element_type=F32)
    for x in range(NX):
        for j in range(BLOCKS):
            columns = slice(j * 128, (j + 1) * 128)
            out_ref[x * BLOCKS + j] = partial[x * DEEP : (x + 1) * DEEP, columns]
            out_ref[x * BLOCKS + j, PART : PART + 1, :] = bias_ref[j : j + 1, :]
            out_ref[x * BLOCKS + j, PART + 1 : PART + 2, :] = second_ref[j : j + 1, :]


def head_kernel(pre_ref, out_ref):
    pre = pre_ref[0]
    for source in range(1, NX * BLOCKS):
        pre = pre + pre_ref[source]
    extra = pre_ref[lax.axis_index("yh") * BLOCKS]
    unit = jnp.maximum(pre + extra[PART : PART + 1, :], 0.0) * extra[PART + 1 : PART + 2, :]
    unit = jnp.where(iota(unit.shape, 0) < PART, unit, 0.0)
    unit = jnp.concatenate([unit, jnp.zeros((128 - DEEP, 128), F32)], axis=0)
    logit = lax.dot_general(
        jnp.ones((8, 128), F32), unit, (((1,), (1,)), ((), ())), precision=HIGH, preferred_element_type=F32
    )
    out_ref[...] = jnp.broadcast_to(logit[0:1, :].reshape(1, 1, 128), out_ref.shape)


def finish_kernel(share_ref, place_ref, before_ref, valid_ref, pairs_ref, logit_ref, reward_ref, score_ref, margin_ref):
    each = share_ref.shape[0] // (NZH * NX)
    rows = []
    for group in range(NZH * NX):
        shares = share_ref[group * each : (group + 1) * each].reshape(each, 128)
        rows.append(jnp.sum(shares, axis=0, keepdims=True))
    table = jnp.concatenate(rows, axis=0)
    place = place_ref[...]
    traces, steps = place.shape
    logits = []
    for t in range(traces):
        row, lane = place[t : t + 1, :] >> 7, place[t : t + 1, :] & 127
        spread = ones_where(iota((128, steps), 0) == lane)
        found = jnp.dot(table, spread, precision=HIGH, preferred_element_type=F32)
        found = jnp.where(iota(found.shape, 0) == row, found, 0.0)
        logits.append(jnp.sum(found, axis=0, keepdims=True))
    logit = before_ref[...] + jnp.concatenate(logits, axis=0)
    logit_ref[...] = logit
    live = valid_ref[...] == 1
    reward_ref[...] = jnp.where(live, logit, 0.0)
    score = jnp.min(jnp.where(live, logit, 1e30), axis=1, keepdims=True)
    diagonal = iota((traces, traces), 0) == iota((traces, traces), 1)
    flat = jnp.sum(jnp.where(diagonal, score, 0.0), axis=0, keepdims=True)
    score_ref[...] = flat
    trace = iota((traces, traces), 1)
    pairs = pairs_ref[...]
    ends = []
    for e in range(2):
        ends.append(jnp.sum(jnp.where(pairs[:, e : e + 1] == trace, flat, 0.0), axis=1, keepdims=True))
    margin_ref[...] = jnp.sum(jnp.where(diagonal, ends[0] - ends[1], 0.0), axis=0, keepdims=True)


def call(kernel, shapes, *args, scalars=0):
    single = not isinstance(shapes, list)
    return pl.pallas_call(
        kernel,
        out_shape=shapes,
        in_specs=[SMEM] * scalars + [VMEM] * (len(args) - scalars),
        out_specs=VMEM if single else [VMEM] * len(shapes),
        compiler_params=pltpu.CompilerParams(vmem_limit_bytes=16 << 20),
        name=kernel.__name__,
    )(*args)


def array(shape, dtype=F32):
    return jax.ShapeDtypeStruct(shape, dtype)


def exchange(pieces, axes):
    return lax.all_to_all(pieces, axes, split_axis=0, concat_axis=0, tiled=True)


def per_device(hidden_states, boundary, valid, pairs, w_first, b_first, w_second):
    columns = w_first.shape[1]
    weight = jnp.pad(w_first, ((0, DEEP - w_first.shape[0]), (0, 0)))
    swap = [(a * NX + b, b * NX + a) for a in range(NYH) for b in range(NX)]
    weight = lax.ppermute(weight, ("yh", "x"), swap)
    weight = lax.all_gather(weight, "zh")
    bias, second = b_first.reshape(8, columns // 8), w_second.reshape(8, columns // 8)

    owner = (boundary >> 6).reshape(-1)
    live = valid.reshape(-1) == 1
    order = jnp.arange(owner.shape[0], dtype=I32)
    same = (owner[:, None] == owner[None, :]) & live[None, :]
    rank = jnp.sum(same & (order[None, :] < order[:, None]), axis=1, dtype=I32)
    most = jnp.max(jnp.where(live, rank + 1, 0))
    group = group_of(owner)
    crowd = jnp.max(jnp.sum((group[:, None] == group[None, :]) & live[None, :], axis=1, dtype=I32))
    first_window = jnp.where((most <= SLOTS) & (crowd <= CAP), SLOTS, ROUND_SLOTS).astype(I32)

    def one_round(numbers, low, window, before):
        picks = call(
            pick_kernel, array((OWNERS, SLOTS, 128), BF16), numbers, boundary, valid, hidden_states, scalars=1
        )
        picks = exchange(picks, ("yh", "y0", "z0", "c"))
        pre = call(
            layer_kernel, array((NX * BLOCKS, DEEP, 128)),
            numbers, boundary, valid, picks, weight, bias, second, scalars=1,
        )
        pre = exchange(pre, ("x", "y0", "z0", "c"))
        share = call(head_kernel, array((NYH * NX * BLOCKS * NZH, 1, 128)), pre)
        share = exchange(share, ("zh", "x", "yh", "y0", "z0", "c"))
        inside = live & (rank >= low) & (rank < low + window)
        ahead = inside[None, :] & (group[None, :] == group[:, None]) & (owner[None, :] < owner[:, None])
        g = jnp.sum(ahead, axis=1, dtype=I32) + rank - low
        place = (group * NX + g // PART) * 128 + g % PART
        place = jnp.where(inside, place, -128).reshape(boundary.shape)
        return call(
            finish_kernel, [array(boundary.shape), array(boundary.shape), array((1, 8)), array((1, 8))],
            share, place, before, valid, pairs,
        )

    first = jnp.array([0, 0], I32)
    found = one_round(first, 0, first_window, jnp.zeros(boundary.shape, F32))

    def more(state):
        low, found = state
        numbers = jnp.stack([low, jnp.int32(ROUND_SLOTS)])
        return low + ROUND_SLOTS, one_round(numbers, low, ROUND_SLOTS, found[0])

    _, found = lax.while_loop(lambda state: state[0] < most, more, (first_window, found))
    return found[1], found[2].reshape(8), found[3].reshape(8)


def solution(mesh):
    torus = Mesh(mesh.devices.reshape(NYH, NY0, NZH, NZ0, NC, NX), NAMES)
    return jax.shard_map(
        per_device,
        mesh=torus,
        in_specs=(P(None, SEQ, "x"), P(), P(), P(), P(SEQ, "x"), P("x"), P("x")),
        out_specs=(P(), P(), P()),
        check_vma=False,
    )
```

time: 176 us -> 91.1 us (0.52)
  waiting for transfers between devices: 81.7 us -> 23 us
  starting transfers between devices: 5 us -> 35.8 us
  blocking collectives: 42.3 us -> 17 us
  local copies, waits for them, and re-layouts: 21.9 us -> 2.95 us
  between operations: 14.1 us -> 2.09 us
  matrix products: 8.25 us -> 0 us
  Pallas kernels: 0 us -> 6.82 us
    all_gather x1 -> x0, waiting for transfers between devices: 43.5 us -> none  [score_rows(): lax.all_gather(w_first, SEQ, axis=0, tiled=True)]
    psum x4 -> x0, blocking collectives: 42.3 us -> none  [over_axes(): shard = lax.psum(shard, axis)]
    all_to_all x1 -> x3, starting transfers between devices: 4.96 us -> 35.1 us  [exchange(): return lax.all_to_all(pieces, axes, split_axis=0, concat_axis=0, tiled=True)]
    all_gather x0 -> x1, blocking collectives: none -> 17 us  [per_device(): weight = lax.all_gather(weight, 'zh')]
    all_to_all x1 -> x3, waiting for transfers between devices: 37.6 us -> 23 us  [exchange(): return lax.all_to_all(pieces, axes, split_axis=0, concat_axis=0, tiled=True)]
    unnamed x14 -> x15, local copies, waits for them, and re-layouts: 13.4 us -> 1.37 us
    dot_general x1 -> x0, matrix products: 8.25 us -> none  [score_rows(): jnp.dot(rows, lax.all_gather(w_first, SEQ, axis=0, tiled=True), preferred...]
    pallas_call x0 -> x4, Pallas kernels: none -> 6.82 us  [call(): pl.pallas_call(kernel, out_shape=shapes, in_specs=[SMEM] * scalars + [VME...]
  transfers between devices with their start and end apart: 2 -> 4, of which waited for: 2 -> 2; matrix products, arithmetic and copies ran while one was open for 6% -> 3% of each run, Pallas kernels for 0% -> 3%
where the time goes in v2:
time: 91.1 us; the launch traced here: 90.6 us
  starting transfers between devices  35.8 us (39%)
  waiting for transfers between devices  23 us (25%)
  blocking collectives  17 us (19%)
  Pallas kernels  6.82 us (7%)
  local copies, waits for them, and re-layouts  2.95 us (3%)
  other arithmetic  2.29 us (3%)
  between operations  2.09 us (2%)
    all_to_all x3, starting transfers between devices, exchange(): return lax.all_to_all(pieces, axes, split_axis=0, concat_axis=0, tiled=True)  35.1 us
    all_to_all x3, waiting for transfers between devices, exchange(): return lax.all_to_all(pieces, axes, split_axis=0, concat_axis=0, tiled=True)  23 us
    all_gather x1, blocking collectives, per_device(): weight = lax.all_gather(weight, 'zh')  17 us
    pallas_call x4, Pallas kernels, call(): pl.pallas_call(kernel, out_shape=shapes, in_specs=[SMEM] * scalars + [VME...  6.82 us
  transfers between devices with their start and end apart: 4, of which 2 were waited for; matrix products, arithmetic and copies ran while one was open for 3% of the time, Pallas kernels for 3%

profile of v2, /device:TPU:1, one launch (start us, length us, event | category | flops | bytes accessed | tf_op | source)
XLA Modules:
  0.0 90.6 jit_solution(17576256014441261573)
XLA Ops:
  0.6 0.0 copy-start.2
  0.6 0.9 pad.4
  1.5 0.0 copy-start.1
  1.5 0.7 collective-permute-start
  2.2 0.0 copy-done.2
  2.2 0.0 copy-start.5
  2.2 0.0 copy-done.1
  2.2 2.5 %pick_kernel.5 = bf16[32,16,128]{2,1,0:T(8,128)(2,1)} custom-call(s32[2]{0:T(128)S(1)} %call_exported.0.round_ref, s32[8,64]{1,0:T(8,128)S(1)} %copy-done.2, s32[8,64]{1,0:T(8,128)S(1)} %copy-done.1, bf16[8,64,896]{2,1,0:T(8,128)(2,1)} %hidden_ref.1), custom_call_target="tpu_custom_call" | custom-call | tf_op jit(solution)/shard_map/pick_kernel/pallas_call | solution.py:155
  4.8 14.5 %all-to-all-start.3 = ((bf16[32,16,128]{2,1,0:T(8,128)(2,1)}), bf16[32,16,128]{2,1,0:T(8,128)(2,1)S(1)}, u32[]{:S(2)}, u32[]{:S(2)}) async-start(bf16[32,16,128]{2,1,0:T(8,128)(2,1)} %pick_kernel.5), calls=%async_computation.3 | async-start | bytes 262144 | tf_op jit(solution)/shard_map/all_to_all | solution.py:170
  19.3 0.1 eq.81
  19.3 0.1 eq.85
  19.4 0.0 collective-permute-done
  19.4 0.0 copy-start.4
  19.4 17.0 %all-gather = bf16[128,1024]{1,0:T(8,128)(2,1)S(1)} all-gather(bf16[32,1024]{1,0:T(8,128)(2,1)S(1)} %collective-permute-done), channel_id=2, replica_groups=mesh['yh'=4,'y0'=2,'zh'=4,'z0'=2,'c'=2,'x'=4] {'zh'}, dimensions={0}, use_global_device_ids=true | all-gather | bytes 327680 | tf_op jit(solution)/shard_map/all_gather | solution.py:178
  36.4 0.0 copy-start.3
  36.4 0.0 all-to-all-done.3.picks_ref
  36.4 0.0 copy-done.4
  36.4 0.7 copy-done.3
  37.1 1.9 %layer_kernel.5 = f32[32,32,128]{2,1,0:T(8,128)} custom-call(s32[2]{0:T(128)S(1)} %call_exported.0.round_ref, s32[8,64]{1,0:T(8,128)S(1)} %copy-done.2, s32[8,64]{1,0:T(8,128)S(1)} %copy-done.1, bf16[32,16,128]{2,1,0:T(8,128)(2,1)S(1)} %all-to-all-done.3.picks_ref, bf16[4,32,1024]{2,1,0:T(8,128)(2,1)S(1)} %bitcast.9, f32[8,128]{1,0:T(8,128)S(1)} %bitcast.11, ...), custom_call_target="tpu_custom_call" | custom-call | tf_op jit(solution)/shard_map/layer_kernel/pallas_call | solution.py:155
  39.0 8.0 %all-to-all-start.4 = ((f32[32,32,128]{2,1,0:T(8,128)}), f32[32,32,128]{2,1,0:T(8,128)S(1)}, u32[]{:S(2)}, u32[]{:S(2)}) async-start(f32[32,32,128]{2,1,0:T(8,128)} %layer_kernel.5), calls=%async_computation.4 | async-start | bytes 1048576 | tf_op jit(solution)/shard_map/all_to_all | solution.py:170
  47.0 0.0 copy-start
  47.0 0.5 convert_reduce_fusion.2
  47.5 0.1 add.76
  47.6 0.7 select_reduce_fusion
  48.9 0.6 reduce_max.19
  50.2 0.5 convert_reduce_fusion.1
  50.6 7.5 %all-to-all-done.4.pre_ref = f32[32,32,128]{2,1,0:T(8,128)S(1)} async-done(((f32[32,32,128]{2,1,0:T(8,128)}), f32[32,32,128]{2,1,0:T(8,128)S(1)}, u32[]{:S(2)}, u32[]{:S(2)}) %all-to-all-start.4) | async-done | bytes 524320 | tf_op jit(solution)/shard_map/all_to_all | solution.py:170
  58.1 1.0 %head_kernel.5 = f32[512,1,128]{2,1,0:T(1,128)} custom-call(f32[32,32,128]{2,1,0:T(8,128)S(1)} %all-to-all-done.4.pre_ref), custom_call_target="tpu_custom_call" | custom-call | tf_op jit(solution)/shard_map/head_kernel/pallas_call | solution.py:155
  59.1 12.7 %all-to-all-start.5 = ((f32[512,1,128]{2,1,0:T(1,128)}), f32[512,1,128]{2,1,0:T(1,128)S(1)}, u32[]{:S(2)}, u32[]{:S(2)}) async-start(f32[512,1,128]{2,1,0:T(1,128)} %head_kernel.5), calls=%async_computation.5 | async-start | bytes 524288 | tf_op jit(solution)/shard_map/all_to_all | solution.py:170
  71.8 0.0 copy-done.5
  71.8 0.1 lt.134
  71.9 0.1 div.24
  72.0 0.1 rem.46
  72.1 0.1 ne.67
  72.1 0.1 lt.104
  72.2 0.0 copy-start.6
  72.2 0.1 ge.31
  72.3 0.6 copy-done.6
  72.9 0.1 copy.13.pairs_ref
  73.0 15.5 %all-to-all-done.5.share_ref = f32[512,1,128]{2,1,0:T(1,128)S(1)} async-done(((f32[512,1,128]{2,1,0:T(1,128)}), f32[512,1,128]{2,1,0:T(1,128)S(1)}, u32[]{:S(2)}, u32[]{:S(2)}) %all-to-all-start.5) | async-done | bytes 262176 | tf_op jit(solution)/shard_map/all_to_all | solution.py:170
  88.6 1.4 %finish_kernel.5 = (f32[8,64]{1,0:T(8,128)S(1)}, f32[8,64]{1,0:T(8,128)}, f32[1,8]{1,0:T(1,128)}, f32[1,8]{1,0:T(1,128)}) custom-call(f32[512,1,128]{2,1,0:T(1,128)S(1)} %all-to-all-done.5.share_ref, s32[8,64]{1,0:T(8,128)S(1)} %fusion.8.place_ref, f32[8,64]{1,0:T(8,128)S(1)} %broadcast_in_dim.31.before_ref, s32[8,64]{1,0:T(8,128)S(1)} %copy-done.1, ...), custom_call_target="tpu_custom_call" | custom-call | tf_op jit(solution)/shard_map/finish_kernel/pallas_call | solution.py:155
  89.9 0.0 copy-done
  89.9 0.6 while.19
  (10 shorter events, 0.1 us)
Async XLA Ops:
  0.6 1.5 %copy-start.2 = (s32[8,64]{1,0:T(8,128)S(1)}, s32[8,64]{1,0:T(8,128)}, u32[]{:S(2)}) copy-start(s32[8,64]{1,0:T(8,128)} %boundary_ref.3) | copy-start | bytes 6148
  1.5 0.7 copy-start.1
  1.5 17.9 %collective-permute-start = (bf16[32,1024]{1,0:T(8,128)(2,1)S(1)}, bf16[32,1024]{1,0:T(8,128)(2,1)S(1)}, u32[]{:S(2)}, u32[]{:S(2)}) collective-permute-start(bf16[32,1024]{1,0:T(8,128)(2,1)S(1)} %pad.4), channel_id=1, source_target_pairs={{0,0},{1,128},{2,256},{3,384},{128,1},{129,129},{130,257},{131,385... | collective-permute-start | bytes 196616 | tf_op jit(solution)/shard_map/ppermute | solution.py:177
  2.2 69.6 %copy-start.5 = (s32[8,64]{1,0:T(8,128)}, s32[8,64]{1,0:T(8,128)S(1)}, u32[]{:S(2)}) copy-start(s32[8,64]{1,0:T(8,128)S(1)} %broadcast_shift-right-arithmetic_fusion) | copy-start | bytes 6148
  4.8 31.7 %all-to-all-start.3 = ((bf16[32,16,128]{2,1,0:T(8,128)(2,1)}), bf16[32,16,128]{2,1,0:T(8,128)(2,1)S(1)}, u32[]{:S(2)}, u32[]{:S(2)}) async-start(bf16[32,16,128]{2,1,0:T(8,128)(2,1)} %pick_kernel.5), calls=%async_computation.3 | async-start | bytes 262144 | tf_op jit(solution)/shard_map/all_to_all | solution.py:170
  19.4 17.0 %copy-start.4 = (f32[1024]{0:T(1024)S(1)}, f32[1024]{0:T(1024)}, u32[]{:S(2)}) copy-start(f32[1024]{0:T(1024)} %param.16) | copy-start | bytes 12292
  36.4 0.7 copy-start.3
  39.0 19.1 %all-to-all-start.4 = ((f32[32,32,128]{2,1,0:T(8,128)}), f32[32,32,128]{2,1,0:T(8,128)S(1)}, u32[]{:S(2)}, u32[]{:S(2)}) async-start(f32[32,32,128]{2,1,0:T(8,128)} %layer_kernel.5), calls=%async_computation.4 | async-start | bytes 1048576 | tf_op jit(solution)/shard_map/all_to_all | solution.py:170
  47.0 42.9 %copy-start = (bf16[8,64,896]{2,1,0:T(8,128)(2,1)S(1)}, bf16[8,64,896]{2,1,0:T(8,128)(2,1)}, u32[]{:S(2)}) copy-start(bf16[8,64,896]{2,1,0:T(8,128)(2,1)} %hidden_ref.1) | copy-start | bytes 2752516
  59.1 29.4 %all-to-all-start.5 = ((f32[512,1,128]{2,1,0:T(1,128)}), f32[512,1,128]{2,1,0:T(1,128)S(1)}, u32[]{:S(2)}, u32[]{:S(2)}) async-start(f32[512,1,128]{2,1,0:T(1,128)} %head_kernel.5), calls=%async_computation.5 | async-start | bytes 524288 | tf_op jit(solution)/shard_map/all_to_all | solution.py:170
  72.2 0.7 copy-start.6

commit v3 on v2

--- a/solution.py
+++ b/solution.py
@@ -32,6 +32,12 @@
 
 def group_of(owner):
     return (owner >> 2) & 3
+
+
+def first_pick_kernel(round_ref, boundary_ref, valid_ref, hidden_ref, bias_ref, second_ref, out_ref, extra_ref):
+    extra_ref[0] = bias_ref[...]
+    extra_ref[1] = second_ref[...]
+    pick_kernel(round_ref, boundary_ref, valid_ref, hidden_ref, out_ref)
 
 
 def pick_kernel(round_ref, boundary_ref, valid_ref, hidden_ref, out_ref):
@@ -58,7 +64,7 @@
     for y0 in range(NY0):
         for low2 in range(NZ0 * NC):
             parts = []
-            for zh in range(NZH):
+            for zh in (0, 3, 2, 1):
                 start = (y0 * 16 + zh * 4 + low2) * depth
                 parts += [picked[:, start : start + depth], pad]
             piece = jnp.concatenate(parts, axis=1).astype(BF16)
@@ -66,7 +72,7 @@
                 out_ref[yh * BLOCKS + y0 * 4 + low2] = piece
 
 
-def layer_kernel(round_ref, boundary_ref, valid_ref, picks_ref, weight_ref, bias_ref, second_ref, out_ref):
+def layer_kernel(round_ref, boundary_ref, valid_ref, picks_ref, extra_ref, w0_ref, w1_ref, w2_ref, w3_ref, out_ref):
     low, window = round_ref[0], round_ref[1]
     traces, steps = boundary_ref.shape
     owner = jnp.where(valid_ref[...] == 1, boundary_ref[...] >> 6, -1)
@@ -77,12 +83,13 @@
     device = iota((128, 1), 0)
     most = jnp.max(count, axis=0, keepdims=True)
     fits = most <= SLOTS
-    for zh in range(NZH):
-        crowd = jnp.sum(jnp.where(group_of(device) == zh, count, 0.0), axis=0, keepdims=True)
+    for group in range(NZH):
+        crowd = jnp.sum(jnp.where(group_of(device) == group, count, 0.0), axis=0, keepdims=True)
         fits = fits & (crowd <= CAP)
     top = jnp.where(window > 0, window.astype(F32), jnp.where(fits, float(SLOTS), float(ROUND_SLOTS)))
     count = jnp.clip(count - low.astype(F32), 0.0, top)
-    mine = group_of(device) == lax.axis_index("zh")
+    zh = lax.axis_index("zh")
+    mine = group_of(device) == zh
     count = jnp.where(mine, count, 0.0)
     place_in_group = (device >> 4) * 4 + (device & 3)
     lane = iota((128, OWNERS * SLOTS), 1) >> 4
@@ -94,21 +101,25 @@
     g = jnp.where(slot < number, g, -1)
     choose = ones_where(g == iota((NX * DEEP, OWNERS * SLOTS), 0), BF16)
     rows = jnp.dot(choose, picks_ref[...].reshape(OWNERS * SLOTS, 128), preferred_element_type=F32)
-    weight = weight_ref[...].reshape(NZH * DEEP, weight_ref.shape[2])
-    partial = jnp.dot(rows.astype(BF16), weight, preferred_element_type=F32)
+    rows = pltpu.roll(rows, zh * DEEP, 1)
+    pad = jnp.zeros((DEEP - w0_ref.shape[0], w0_ref.shape[1]), BF16)
+    weight = []
+    for ref in (w0_ref, w1_ref, w2_ref, w3_ref):
+        weight += [ref[...], pad]
+    partial = jnp.dot(rows.astype(BF16), jnp.concatenate(weight, axis=0), preferred_element_type=F32)
     for x in range(NX):
         for j in range(BLOCKS):
             columns = slice(j * 128, (j + 1) * 128)
             out_ref[x * BLOCKS + j] = partial[x * DEEP : (x + 1) * DEEP, columns]
-            out_ref[x * BLOCKS + j, PART : PART + 1, :] = bias_ref[j : j + 1, :]
-            out_ref[x * BLOCKS + j, PART + 1 : PART + 2, :] = second_ref[j : j + 1, :]
+            out_ref[x * BLOCKS + j, PART : PART + 1, :] = extra_ref[0, j : j + 1, :]
+            out_ref[x * BLOCKS + j, PART + 1 : PART + 2, :] = extra_ref[1, j : j + 1, :]
 
 
 def head_kernel(pre_ref, out_ref):
     pre = pre_ref[0]
     for source in range(1, NX * BLOCKS):
         pre = pre + pre_ref[source]
-    extra = pre_ref[lax.axis_index("yh") * BLOCKS]
+    extra = pre_ref[lax.rem(lax.axis_index("yh") + 2, NX) * BLOCKS]
     unit = jnp.maximum(pre + extra[PART : PART + 1, :], 0.0) * extra[PART + 1 : PART + 2, :]
     unit = jnp.where(iota(unit.shape, 0) < PART, unit, 0.0)
     unit = jnp.concatenate([unit, jnp.zeros((128 - DEEP, 128), F32)], axis=0)
@@ -116,6 +127,10 @@
         jnp.ones((8, 128), F32), unit, (((1,), (1,)), ((), ())), precision=HIGH, preferred_element_type=F32
     )
     out_ref[...] = jnp.broadcast_to(logit[0:1, :].reshape(1, 1, 128), out_ref.shape)
+
+
+def spread_kernel(share_ref, out_ref):
+    out_ref[...] = jnp.broadcast_to(jnp.sum(share_ref[...], axis=0, keepdims=True), out_ref.shape)
 
 
 def finish_kernel(share_ref, place_ref, before_ref, valid_ref, pairs_ref, logit_ref, reward_ref, score_ref, margin_ref):
@@ -172,10 +187,10 @@
 
 def per_device(hidden_states, boundary, valid, pairs, w_first, b_first, w_second):
     columns = w_first.shape[1]
-    weight = jnp.pad(w_first, ((0, DEEP - w_first.shape[0]), (0, 0)))
-    swap = [(a * NX + b, b * NX + a) for a in range(NYH) for b in range(NX)]
-    weight = lax.ppermute(weight, ("yh", "x"), swap)
-    weight = lax.all_gather(weight, "zh")
+    swap = [(a * NX + b, (b + 2) % NYH * NX + a) for a in range(NYH) for b in range(NX)]
+    weights = [lax.ppermute(w_first, ("yh", "x"), swap)]
+    for k in range(1, NZH):
+        weights.append(lax.ppermute(weights[0], "zh", [(i, (i + k) % NZH) for i in range(NZH)]))
     bias, second = b_first.reshape(8, columns // 8), w_second.reshape(8, columns // 8)
 
     owner = (boundary >> 6).reshape(-1)
@@ -188,18 +203,18 @@
     crowd = jnp.max(jnp.sum((group[:, None] == group[None, :]) & live[None, :], axis=1, dtype=I32))
     first_window = jnp.where((most <= SLOTS) & (crowd <= CAP), SLOTS, ROUND_SLOTS).astype(I32)
 
-    def one_round(numbers, low, window, before):
-        picks = call(
-            pick_kernel, array((OWNERS, SLOTS, 128), BF16), numbers, boundary, valid, hidden_states, scalars=1
-        )
+    shape = array((OWNERS, SLOTS, 128), BF16)
+
+    def one_round(numbers, low, window, before, picks, extra):
         picks = exchange(picks, ("yh", "y0", "z0", "c"))
         pre = call(
             layer_kernel, array((NX * BLOCKS, DEEP, 128)),
-            numbers, boundary, valid, picks, weight, bias, second, scalars=1,
+            numbers, boundary, valid, picks, extra, *weights, scalars=1,
         )
         pre = exchange(pre, ("x", "y0", "z0", "c"))
-        share = call(head_kernel, array((NYH * NX * BLOCKS * NZH, 1, 128)), pre)
-        share = exchange(share, ("zh", "x", "yh", "y0", "z0", "c"))
+        share = exchange(call(head_kernel, array((NYH * NY0, 1, 128)), pre), ("yh", "y0"))
+        share = call(spread_kernel, array((NZH * NX * NZ0 * NC, 1, 128)), share)
+        share = exchange(share, ("zh", "x", "z0", "c"))
         inside = live & (rank >= low) & (rank < low + window)
         ahead = inside[None, :] & (group[None, :] == group[:, None]) & (owner[None, :] < owner[:, None])
         g = jnp.sum(ahead, axis=1, dtype=I32) + rank - low
@@ -211,12 +226,17 @@
         )
 
     first = jnp.array([0, 0], I32)
-    found = one_round(first, 0, first_window, jnp.zeros(boundary.shape, F32))
+    picks, extra = call(
+        first_pick_kernel, [shape, array((2, 8, 128))],
+        first, boundary, valid, hidden_states, bias, second, scalars=1,
+    )
+    found = one_round(first, 0, first_window, jnp.zeros(boundary.shape, F32), picks, extra)
 
     def more(state):
         low, found = state
         numbers = jnp.stack([low, jnp.int32(ROUND_SLOTS)])
-        return low + ROUND_SLOTS, one_round(numbers, low, ROUND_SLOTS, found[0])
+        picks = call(pick_kernel, shape, numbers, boundary, valid, hidden_states, scalars=1)
+        return low + ROUND_SLOTS, one_round(numbers, low, ROUND_SLOTS, found[0], picks, extra)
 
     _, found = lax.while_loop(lambda state: state[0] < most, more, (first_window, found))
     return found[1], found[2].reshape(8), found[3].reshape(8)

time: 91.1 us -> 93.8 us (1.030)
  starting transfers between devices: 35.8 us -> 53.4 us
  blocking collectives: 17 us -> 0 us
  waiting for transfers between devices: 23 us -> 24.7 us
    ppermute x1 -> x4, starting transfers between devices: 0.66 us -> 25.5 us  [the longest x3 17.3 us: per_device(): lax.ppermute(weights[0], 'zh', [(i, (i + k) % NZH) for i in range(NZH)])]
    all_gather x1 -> x0, blocking collectives: 17 us -> none  [per_device(): weight = lax.all_gather(weight, 'zh')]
    all_to_all x3 -> x4, starting transfers between devices: 35.1 us -> 27.9 us  [exchange(): return lax.all_to_all(pieces, axes, split_axis=0, concat_axis=0, tiled=True)]
    ppermute x1 -> x4, waiting for transfers between devices: 0.01 us -> 2.43 us  [the longest x3 2.43 us: per_device(): lax.ppermute(weights[0], 'zh', [(i, (i + k) % NZH) for i in range(NZH)])]
    all_to_all x3 -> x4, waiting for transfers between devices: 23 us -> 22.2 us  [exchange(): return lax.all_to_all(pieces, axes, split_axis=0, concat_axis=0, tiled=True)]
    pallas_call x4 -> x5, Pallas kernels: 6.82 us -> 7.2 us  [call(): pl.pallas_call(kernel, out_shape=shapes, in_specs=[SMEM] * scalars + [VME...]
  transfers between devices with their start and end apart: 4 -> 8, of which waited for: 2 -> 5; matrix products, arithmetic and copies ran while one was open for 3% -> 4% of each run, Pallas kernels for 3% -> 3%
where the time goes in v3:
time: 93.8 us; the launch traced here: 93.1 us
  starting transfers between devices  53.4 us (57%)
  waiting for transfers between devices  24.7 us (26%)
  Pallas kernels  7.2 us (8%)
  other arithmetic  2.99 us (3%)
  local copies, waits for them, and re-layouts  2.09 us (2%)
  between operations  2.09 us (2%)
    all_to_all x4, starting transfers between devices, exchange(): return lax.all_to_all(pieces, axes, split_axis=0, concat_axis=0, tiled=True)  27.9 us
    all_to_all x4, waiting for transfers between devices, exchange(): return lax.all_to_all(pieces, axes, split_axis=0, concat_axis=0, tiled=True)  22.2 us
    ppermute x3, starting transfers between devices, per_device(): lax.ppermute(weights[0], 'zh', [(i, (i + k) % NZH) for i in range(NZH)])  17.3 us
    ppermute x1, starting transfers between devices, per_device(): weights = [lax.ppermute(w_first, ('yh', 'x'), swap)]  8.27 us
    pallas_call x5, Pallas kernels, call(): pl.pallas_call(kernel, out_shape=shapes, in_specs=[SMEM] * scalars + [VME...  7.2 us
    ppermute x3, waiting for transfers between devices, per_device(): lax.ppermute(weights[0], 'zh', [(i, (i + k) % NZH) for i in range(NZH)])  2.43 us
  transfers between devices with their start and end apart: 8, of which 5 were waited for; matrix products, arithmetic and copies ran while one was open for 4% of the time, Pallas kernels for 3%

profile of v3, /device:TPU:1, one launch (start us, length us, event | category | flops | bytes accessed | tf_op | source)
XLA Modules:
  0.0 93.1 jit_solution(5152300978678362397)
XLA Ops:
  0.6 8.3 %collective-permute-start = (bf16[28,1024]{1,0:T(8,128)(2,1)}, bf16[28,1024]{1,0:T(8,128)(2,1)S(1)}, u32[]{:S(2)}, u32[]{:S(2)}) collective-permute-start(bf16[28,1024]{1,0:T(8,128)(2,1)} %param.14), channel_id=1, source_target_pairs={{0,256},{1,384},{2,0},{3,128},{128,257},{129,385},{130,1},{131,129... | collective-permute-start | bytes 172040 | tf_op jit(solution)/shard_map/ppermute | solution.py:191
  8.9 0.0 copy-start.1
  8.9 0.0 copy-start.3
  8.9 0.7 broadcast_shift-right-arithmetic_fusion
  9.6 0.0 copy-start
  9.6 0.0 copy-done.1
  9.6 0.0 copy-done.3
  9.7 0.7 copy-done
  10.3 2.6 %first_pick_kernel.1 = (bf16[32,16,128]{2,1,0:T(8,128)(2,1)}, f32[2,8,128]{2,1,0:T(8,128)S(1)}) custom-call(s32[2]{0:T(128)S(1)} %call_exported.0.round_ref, s32[8,64]{1,0:T(8,128)} %boundary_ref.3, s32[8,64]{1,0:T(8,128)S(1)} %copy-done.3, bf16[8,64,896]{2,1,0:T(8,128)(2,1)} %hidden_ref.1, f32[8,128]{1,0:T(8,128)S(1)} %bitcast.8, f32[8,128]{1,0:T(8,128)S(1)} %bitcast.9), custom_call_target="tpu_custom_call" | custom-call | tf_op jit(solution)/shard_map/first_pick_kernel/pallas_call | solution.py:170
  12.9 7.2 %all-to-all-start.4 = ((bf16[32,16,128]{2,1,0:T(8,128)(2,1)}), bf16[32,16,128]{2,1,0:T(8,128)(2,1)S(1)}, u32[]{:S(2)}, u32[]{:S(2)}) async-start(bf16[32,16,128]{2,1,0:T(8,128)(2,1)} %get-tuple-element.239), calls=%async_computation.4 | async-start | bytes 262144 | tf_op jit(solution)/shard_map/all_to_all | solution.py:185
  20.1 0.1 eq.81
  20.2 0.0 collective-permute-done.w0_ref
  20.2 5.9 %collective-permute-start.1 = (bf16[28,1024]{1,0:T(8,128)(2,1)S(1)}, bf16[28,1024]{1,0:T(8,128)(2,1)S(1)}, u32[]{:S(2)}, u32[]{:S(2)}) collective-permute-start(bf16[28,1024]{1,0:T(8,128)(2,1)S(1)} %collective-permute-done.w0_ref), channel_id=1, source_target_pairs={{0,16},{16,32},{32,48},{48,0},{1,17},{17,33},{33,49},{49,1},{2,18}... | collective-permute-start | bytes 172040 | tf_op jit(solution)/shard_map/ppermute | solution.py:193
  26.1 7.9 %collective-permute-start.2 = (bf16[28,1024]{1,0:T(8,128)(2,1)S(1)}, bf16[28,1024]{1,0:T(8,128)(2,1)S(1)}, u32[]{:S(2)}, u32[]{:S(2)}) collective-permute-start(bf16[28,1024]{1,0:T(8,128)(2,1)S(1)} %collective-permute-done.w0_ref), channel_id=1, source_target_pairs={{0,32},{16,48},{32,0},{48,16},{1,33},{17,49},{33,1},{49,17},{2,34}... | collective-permute-start | bytes 172040 | tf_op jit(solution)/shard_map/ppermute | solution.py:193
  34.1 3.4 %collective-permute-start.3 = (bf16[28,1024]{1,0:T(8,128)(2,1)S(1)}, bf16[28,1024]{1,0:T(8,128)(2,1)S(1)}, u32[]{:S(2)}, u32[]{:S(2)}) collective-permute-start(bf16[28,1024]{1,0:T(8,128)(2,1)S(1)} %collective-permute-done.w0_ref), channel_id=1, source_target_pairs={{0,48},{16,0},{32,16},{48,32},{1,49},{17,1},{33,17},{49,33},{2,50}... | collective-permute-start | bytes 172040 | tf_op jit(solution)/shard_map/ppermute | solution.py:193
  37.5 0.1 eq.85
  37.6 0.0 collective-permute-done.1.w1_ref
  37.6 0.2 collective-permute-done.2.w2_ref
  37.7 2.3 %collective-permute-done.3.w3_ref = bf16[28,1024]{1,0:T(8,128)(2,1)S(1)} collective-permute-done((bf16[28,1024]{1,0:T(8,128)(2,1)S(1)}, bf16[28,1024]{1,0:T(8,128)(2,1)S(1)}, u32[]{:S(2)}, u32[]{:S(2)}) %collective-permute-start.3) | collective-permute-done | bytes 57376 | tf_op jit(solution)/shard_map/ppermute | solution.py:193
  40.0 0.0 all-to-all-done.4.picks_ref
  40.0 0.0 copy-done.4
  40.0 2.0 %layer_kernel.5 = f32[32,32,128]{2,1,0:T(8,128)} custom-call(s32[2]{0:T(128)S(1)} %call_exported.0.round_ref, s32[8,64]{1,0:T(8,128)S(1)} %copy-done.4, s32[8,64]{1,0:T(8,128)S(1)} %copy-done.3, bf16[32,16,128]{2,1,0:T(8,128)(2,1)S(1)} %all-to-all-done.4.picks_ref, f32[2,8,128]{2,1,0:T(8,128)S(1)} %get-tuple-element.558.extra_ref, ...), custom_call_target="tpu_custom_call" | custom-call | tf_op jit(solution)/shard_map/layer_kernel/pallas_call | solution.py:170
  42.0 6.6 %all-to-all-start.5 = ((f32[32,32,128]{2,1,0:T(8,128)}), f32[32,32,128]{2,1,0:T(8,128)S(1)}, u32[]{:S(2)}, u32[]{:S(2)}) async-start(f32[32,32,128]{2,1,0:T(8,128)} %layer_kernel.5), calls=%async_computation.5 | async-start | bytes 1048576 | tf_op jit(solution)/shard_map/all_to_all | solution.py:185
  48.6 0.5 convert_reduce_fusion.2
  49.1 0.1 add.74
  49.2 0.7 select_reduce_fusion
  50.5 0.6 reduce_max.19
  51.8 0.5 convert_reduce_fusion.1
  52.3 7.6 %all-to-all-done.5.pre_ref = f32[32,32,128]{2,1,0:T(8,128)S(1)} async-done(((f32[32,32,128]{2,1,0:T(8,128)}), f32[32,32,128]{2,1,0:T(8,128)S(1)}, u32[]{:S(2)}, u32[]{:S(2)}) %all-to-all-start.5) | async-done | bytes 524320 | tf_op jit(solution)/shard_map/all_to_all | solution.py:185
  59.9 0.8 head_kernel.5
  60.6 6.4 %all-to-all-start.6 = ((f32[8,1,128]{2,1,0:T(1,128)}), f32[8,1,128]{2,1,0:T(1,128)S(1)}, u32[]{:S(2)}, u32[]{:S(2)}) async-start(f32[8,1,128]{2,1,0:T(1,128)} %head_kernel.5), calls=%async_computation.6 | async-start | bytes 8192 | tf_op jit(solution)/shard_map/all_to_all | solution.py:185
  67.1 0.1 div.24
  67.1 0.1 rem.46
  67.2 0.1 ne.67
  67.3 0.1 lt.104
  67.4 0.1 ge.31
  67.5 6.1 %all-to-all-done.6.share_ref = f32[8,1,128]{2,1,0:T(1,128)S(1)} async-done(((f32[8,1,128]{2,1,0:T(1,128)}), f32[8,1,128]{2,1,0:T(1,128)S(1)}, u32[]{:S(2)}, u32[]{:S(2)}) %all-to-all-start.6) | async-done | bytes 4128 | tf_op jit(solution)/shard_map/all_to_all | solution.py:185
  73.5 0.6 spread_kernel.5
  74.2 7.7 %all-to-all-start.7 = ((f32[64,1,128]{2,1,0:T(1,128)}), f32[64,1,128]{2,1,0:T(1,128)S(1)}, u32[]{:S(2)}, u32[]{:S(2)}) async-start(f32[64,1,128]{2,1,0:T(1,128)} %spread_kernel.5), calls=%async_computation.7 | async-start | bytes 65536 | tf_op jit(solution)/shard_map/all_to_all | solution.py:185
  81.9 0.0 copy-done.5
  81.9 0.0 copy-start.6
  81.9 0.1 lt.134
  81.9 0.6 copy-done.6
  82.5 0.1 copy.13.pairs_ref
  82.6 8.6 %all-to-all-done.7.share_ref = f32[64,1,128]{2,1,0:T(1,128)S(1)} async-done(((f32[64,1,128]{2,1,0:T(1,128)}), f32[64,1,128]{2,1,0:T(1,128)S(1)}, u32[]{:S(2)}, u32[]{:S(2)}) %all-to-all-start.7) | async-done | bytes 32800 | tf_op jit(solution)/shard_map/all_to_all | solution.py:185
  91.2 1.3 %finish_kernel.5 = (f32[8,64]{1,0:T(8,128)S(1)}, f32[8,64]{1,0:T(8,128)}, f32[1,8]{1,0:T(1,128)}, f32[1,8]{1,0:T(1,128)}) custom-call(f32[64,1,128]{2,1,0:T(1,128)S(1)} %all-to-all-done.7.share_ref, s32[8,64]{1,0:T(8,128)S(1)} %fusion.8.place_ref, f32[8,64]{1,0:T(8,128)S(1)} %broadcast_in_dim.31.before_ref, s32[8,64]{1,0:T(8,128)S(1)} %copy-done.3, ...), custom_call_target="tpu_custom_call" | custom-call | tf_op jit(solution)/shard_map/finish_kernel/pallas_call | solution.py:170
  92.5 0.0 copy-done.2
  92.5 0.6 while.19
  (12 shorter events, 0.1 us)
Async XLA Ops:
  0.6 19.6 %collective-permute-start = (bf16[28,1024]{1,0:T(8,128)(2,1)}, bf16[28,1024]{1,0:T(8,128)(2,1)S(1)}, u32[]{:S(2)}, u32[]{:S(2)}) collective-permute-start(bf16[28,1024]{1,0:T(8,128)(2,1)} %param.14), channel_id=1, source_target_pairs={{0,256},{1,384},{2,0},{3,128},{128,257},{129,385},{130,1},{131,129... | collective-permute-start | bytes 172040 | tf_op jit(solution)/shard_map/ppermute | solution.py:191
  8.9 0.7 copy-start.1
  8.9 0.7 copy-start.3
  9.6 72.2 %copy-start.5 = (s32[8,64]{1,0:T(8,128)}, s32[8,64]{1,0:T(8,128)S(1)}, u32[]{:S(2)}) copy-start(s32[8,64]{1,0:T(8,128)S(1)} %broadcast_shift-right-arithmetic_fusion) | copy-start | bytes 6148
  9.6 0.7 copy-start
  12.9 27.1 %all-to-all-start.4 = ((bf16[32,16,128]{2,1,0:T(8,128)(2,1)}), bf16[32,16,128]{2,1,0:T(8,128)(2,1)S(1)}, u32[]{:S(2)}, u32[]{:S(2)}) async-start(bf16[32,16,128]{2,1,0:T(8,128)(2,1)} %get-tuple-element.239), calls=%async_computation.4 | async-start | bytes 262144 | tf_op jit(solution)/shard_map/all_to_all | solution.py:185
  20.2 19.8 %copy-start.4 = (s32[8,64]{1,0:T(8,128)S(1)}, s32[8,64]{1,0:T(8,128)}, u32[]{:S(2)}) copy-start(s32[8,64]{1,0:T(8,128)} %boundary_ref.3) | copy-start | bytes 6148
  20.2 17.4 %collective-permute-start.1 = (bf16[28,1024]{1,0:T(8,128)(2,1)S(1)}, bf16[28,1024]{1,0:T(8,128)(2,1)S(1)}, u32[]{:S(2)}, u32[]{:S(2)}) collective-permute-start(bf16[28,1024]{1,0:T(8,128)(2,1)S(1)} %collective-permute-done.w0_ref), channel_id=1, source_target_pairs={{0,16},{16,32},{32,48},{48,0},{1,17},{17,33},{33,49},{49,1},{2,18}... | collective-permute-start | bytes 172040 | tf_op jit(solution)/shard_map/ppermute | solution.py:193
  26.1 11.6 %collective-permute-start.2 = (bf16[28,1024]{1,0:T(8,128)(2,1)S(1)}, bf16[28,1024]{1,0:T(8,128)(2,1)S(1)}, u32[]{:S(2)}, u32[]{:S(2)}) collective-permute-start(bf16[28,1024]{1,0:T(8,128)(2,1)S(1)} %collective-permute-done.w0_ref), channel_id=1, source_target_pairs={{0,32},{16,48},{32,0},{48,16},{1,33},{17,49},{33,1},{49,17},{2,34}... | collective-permute-start | bytes 172040 | tf_op jit(solution)/shard_map/ppermute | solution.py:193
  34.1 5.9 %collective-permute-start.3 = (bf16[28,1024]{1,0:T(8,128)(2,1)S(1)}, bf16[28,1024]{1,0:T(8,128)(2,1)S(1)}, u32[]{:S(2)}, u32[]{:S(2)}) collective-permute-start(bf16[28,1024]{1,0:T(8,128)(2,1)S(1)} %collective-permute-done.w0_ref), channel_id=1, source_target_pairs={{0,48},{16,0},{32,16},{48,32},{1,49},{17,1},{33,17},{49,33},{2,50}... | collective-permute-start | bytes 172040 | tf_op jit(solution)/shard_map/ppermute | solution.py:193
  42.0 50.5 %copy-start.2 = (bf16[8,64,896]{2,1,0:T(8,128)(2,1)S(1)}, bf16[8,64,896]{2,1,0:T(8,128)(2,1)}, u32[]{:S(2)}) copy-start(bf16[8,64,896]{2,1,0:T(8,128)(2,1)} %hidden_ref.1) | copy-start | bytes 2752516
  42.0 17.9 %all-to-all-start.5 = ((f32[32,32,128]{2,1,0:T(8,128)}), f32[32,32,128]{2,1,0:T(8,128)S(1)}, u32[]{:S(2)}, u32[]{:S(2)}) async-start(f32[32,32,128]{2,1,0:T(8,128)} %layer_kernel.5), calls=%async_computation.5 | async-start | bytes 1048576 | tf_op jit(solution)/shard_map/all_to_all | solution.py:185
  60.6 12.9 %all-to-all-start.6 = ((f32[8,1,128]{2,1,0:T(1,128)}), f32[8,1,128]{2,1,0:T(1,128)S(1)}, u32[]{:S(2)}, u32[]{:S(2)}) async-start(f32[8,1,128]{2,1,0:T(1,128)} %head_kernel.5), calls=%async_computation.6 | async-start | bytes 8192 | tf_op jit(solution)/shard_map/all_to_all | solution.py:185
  74.2 17.1 %all-to-all-start.7 = ((f32[64,1,128]{2,1,0:T(1,128)}), f32[64,1,128]{2,1,0:T(1,128)S(1)}, u32[]{:S(2)}, u32[]{:S(2)}) async-start(f32[64,1,128]{2,1,0:T(1,128)} %spread_kernel.5), calls=%async_computation.7 | async-start | bytes 65536 | tf_op jit(solution)/shard_map/all_to_all | solution.py:185
  81.9 0.7 copy-start.6

commit v4 on v3

--- a/solution.py
+++ b/solution.py
@@ -7,8 +7,9 @@
 from jax.sharding import PartitionSpec as P
 
 NYH, NY0, NZH, NZ0, NC, NX = 4, 2, 4, 2, 2, 4
-NAMES = ("yh", "y0", "zh", "z0", "c", "x")
-SEQ = NAMES[:5]
+NAMES = ("yh", "y0", "z2", "z1", "z0", "c", "x")
+SEQ = NAMES[:6]
+ZH = ("z2", "z1")
 OWNERS = NYH * NY0 * NZ0 * NC
 BLOCKS = NY0 * NZ0 * NC
 SLOTS = 16
@@ -64,7 +65,7 @@
     for y0 in range(NY0):
         for low2 in range(NZ0 * NC):
             parts = []
-            for zh in (0, 3, 2, 1):
+            for zh in range(NZH):
                 start = (y0 * 16 + zh * 4 + low2) * depth
                 parts += [picked[:, start : start + depth], pad]
             piece = jnp.concatenate(parts, axis=1).astype(BF16)
@@ -72,7 +73,7 @@
                 out_ref[yh * BLOCKS + y0 * 4 + low2] = piece
 
 
-def layer_kernel(round_ref, boundary_ref, valid_ref, picks_ref, extra_ref, w0_ref, w1_ref, w2_ref, w3_ref, out_ref):
+def layer_kernel(round_ref, boundary_ref, valid_ref, picks_ref, extra_ref, weight_ref, out_ref):
     low, window = round_ref[0], round_ref[1]
     traces, steps = boundary_ref.shape
     owner = jnp.where(valid_ref[...] == 1, boundary_ref[...] >> 6, -1)
@@ -88,7 +89,7 @@
         fits = fits & (crowd <= CAP)
     top = jnp.where(window > 0, window.astype(F32), jnp.where(fits, float(SLOTS), float(ROUND_SLOTS)))
     count = jnp.clip(count - low.astype(F32), 0.0, top)
-    zh = lax.axis_index("zh")
+    zh = lax.axis_index(ZH)
     mine = group_of(device) == zh
     count = jnp.where(mine, count, 0.0)
     place_in_group = (device >> 4) * 4 + (device & 3)
@@ -101,11 +102,10 @@
     g = jnp.where(slot < number, g, -1)
     choose = ones_where(g == iota((NX * DEEP, OWNERS * SLOTS), 0), BF16)
     rows = jnp.dot(choose, picks_ref[...].reshape(OWNERS * SLOTS, 128), preferred_element_type=F32)
-    rows = pltpu.roll(rows, zh * DEEP, 1)
-    pad = jnp.zeros((DEEP - w0_ref.shape[0], w0_ref.shape[1]), BF16)
+    pad = jnp.zeros((DEEP - weight_ref.shape[1], weight_ref.shape[2]), BF16)
     weight = []
-    for ref in (w0_ref, w1_ref, w2_ref, w3_ref):
-        weight += [ref[...], pad]
+    for source in range(NZH):
+        weight += [weight_ref[(source & 1) * 2 + ((source >> 1) ^ (zh >> 1))], pad]
     partial = jnp.dot(rows.astype(BF16), jnp.concatenate(weight, axis=0), preferred_element_type=F32)
     for x in range(NX):
         for j in range(BLOCKS):
@@ -119,7 +119,7 @@
     pre = pre_ref[0]
     for source in range(1, NX * BLOCKS):
         pre = pre + pre_ref[source]
-    extra = pre_ref[lax.rem(lax.axis_index("yh") + 2, NX) * BLOCKS]
+    extra = pre_ref[lax.axis_index("yh") * BLOCKS]
     unit = jnp.maximum(pre + extra[PART : PART + 1, :], 0.0) * extra[PART + 1 : PART + 2, :]
     unit = jnp.where(iota(unit.shape, 0) < PART, unit, 0.0)
     unit = jnp.concatenate([unit, jnp.zeros((128 - DEEP, 128), F32)], axis=0)
@@ -139,17 +139,14 @@
     for group in range(NZH * NX):
         shares = share_ref[group * each : (group + 1) * each].reshape(each, 128)
         rows.append(jnp.sum(shares, axis=0, keepdims=True))
-    table = jnp.concatenate(rows, axis=0)
     place = place_ref[...]
-    traces, steps = place.shape
-    logits = []
-    for t in range(traces):
-        row, lane = place[t : t + 1, :] >> 7, place[t : t + 1, :] & 127
-        spread = ones_where(iota((128, steps), 0) == lane)
-        found = jnp.dot(table, spread, precision=HIGH, preferred_element_type=F32)
-        found = jnp.where(iota(found.shape, 0) == row, found, 0.0)
-        logits.append(jnp.sum(found, axis=0, keepdims=True))
-    logit = before_ref[...] + jnp.concatenate(logits, axis=0)
+    traces, steps = valid_ref.shape
+    row, lane = place >> 7, place & 127
+    found = jnp.zeros(place.shape, F32)
+    for group in range(NZH * NX):
+        here = jnp.take_along_axis(jnp.broadcast_to(rows[group], place.shape), lane, axis=1)
+        found = jnp.where(row == group, here, found)
+    logit = before_ref[...] + found[:, :steps]
     logit_ref[...] = logit
     live = valid_ref[...] == 1
     reward_ref[...] = jnp.where(live, logit, 0.0)
@@ -187,63 +184,78 @@
 
 def per_device(hidden_states, boundary, valid, pairs, w_first, b_first, w_second):
     columns = w_first.shape[1]
-    swap = [(a * NX + b, (b + 2) % NYH * NX + a) for a in range(NYH) for b in range(NX)]
-    weights = [lax.ppermute(w_first, ("yh", "x"), swap)]
-    for k in range(1, NZH):
-        weights.append(lax.ppermute(weights[0], "zh", [(i, (i + k) % NZH) for i in range(NZH)]))
+    weights = []
+    for flip in range(2):
+        swap = []
+        for a in range(NYH):
+            for z in range(2):
+                swap += [((a * 2 + z) * NX + b, (b * 2 + (z ^ flip)) * NX + a) for b in range(NX)]
+        weights.append(lax.ppermute(w_first, ("yh", "z2", "x"), swap))
+    weight = lax.all_gather(jnp.stack(weights), "z1").reshape(NZH, *w_first.shape)
     bias, second = b_first.reshape(8, columns // 8), w_second.reshape(8, columns // 8)
 
-    owner = (boundary >> 6).reshape(-1)
-    live = valid.reshape(-1) == 1
-    order = jnp.arange(owner.shape[0], dtype=I32)
-    same = (owner[:, None] == owner[None, :]) & live[None, :]
-    rank = jnp.sum(same & (order[None, :] < order[:, None]), axis=1, dtype=I32)
-    most = jnp.max(jnp.where(live, rank + 1, 0))
-    group = group_of(owner)
-    crowd = jnp.max(jnp.sum((group[:, None] == group[None, :]) & live[None, :], axis=1, dtype=I32))
-    first_window = jnp.where((most <= SLOTS) & (crowd <= CAP), SLOTS, ROUND_SLOTS).astype(I32)
+    def ranks(boundary, valid):
+        owner = (boundary >> 6).reshape(-1)
+        live = valid.reshape(-1) == 1
+        order = jnp.arange(owner.shape[0], dtype=I32)
+        same = (owner[:, None] == owner[None, :]) & live[None, :]
+        rank = jnp.sum(same & (order[None, :] < order[:, None]), axis=1, dtype=I32)
+        return owner, live, rank, group_of(owner)
+
+    def limits(owner, live, rank, group):
+        most = jnp.max(jnp.where(live, rank + 1, 0))
+        crowd = jnp.max(jnp.sum((group[:, None] == group[None, :]) & live[None, :], axis=1, dtype=I32))
+        return most, jnp.where((most <= SLOTS) & (crowd <= CAP), SLOTS, ROUND_SLOTS).astype(I32)
 
     shape = array((OWNERS, SLOTS, 128), BF16)
 
     def one_round(numbers, low, window, before, picks, extra):
+        most = None
         picks = exchange(picks, ("yh", "y0", "z0", "c"))
         pre = call(
             layer_kernel, array((NX * BLOCKS, DEEP, 128)),
-            numbers, boundary, valid, picks, extra, *weights, scalars=1,
+            numbers, boundary, valid, picks, extra, weight, scalars=1,
         )
+        pre, late_boundary, late_valid = lax.optimization_barrier((pre, boundary, valid))
+        owner, live, rank, group = ranks(late_boundary, late_valid)
+        if window is None:
+            most, window = limits(owner, live, rank, group)
         pre = exchange(pre, ("x", "y0", "z0", "c"))
-        share = exchange(call(head_kernel, array((NYH * NY0, 1, 128)), pre), ("yh", "y0"))
-        share = call(spread_kernel, array((NZH * NX * NZ0 * NC, 1, 128)), share)
-        share = exchange(share, ("zh", "x", "z0", "c"))
+        share = exchange(call(head_kernel, array((NYH * NY0 * NC, 1, 128)), pre), ("yh", "y0", "c"))
+        share = call(spread_kernel, array((NZH * NX * NZ0, 1, 128)), share)
+        share = exchange(share, ZH + ("x", "z0"))
         inside = live & (rank >= low) & (rank < low + window)
         ahead = inside[None, :] & (group[None, :] == group[:, None]) & (owner[None, :] < owner[:, None])
         g = jnp.sum(ahead, axis=1, dtype=I32) + rank - low
         place = (group * NX + g // PART) * 128 + g % PART
         place = jnp.where(inside, place, -128).reshape(boundary.shape)
-        return call(
+        place = jnp.pad(place, ((0, 0), (0, 128 - boundary.shape[1])), constant_values=-128)
+        found = call(
             finish_kernel, [array(boundary.shape), array(boundary.shape), array((1, 8)), array((1, 8))],
             share, place, before, valid, pairs,
         )
+        return found, most, window
 
     first = jnp.array([0, 0], I32)
     picks, extra = call(
         first_pick_kernel, [shape, array((2, 8, 128))],
         first, boundary, valid, hidden_states, bias, second, scalars=1,
     )
-    found = one_round(first, 0, first_window, jnp.zeros(boundary.shape, F32), picks, extra)
+    found, most, window = one_round(first, 0, None, jnp.zeros(boundary.shape, F32), picks, extra)
 
     def more(state):
         low, found = state
         numbers = jnp.stack([low, jnp.int32(ROUND_SLOTS)])
         picks = call(pick_kernel, shape, numbers, boundary, valid, hidden_states, scalars=1)
-        return low + ROUND_SLOTS, one_round(numbers, low, ROUND_SLOTS, found[0], picks, extra)
-
-    _, found = lax.while_loop(lambda state: state[0] < most, more, (first_window, found))
+        found, _, _ = one_round(numbers, low, ROUND_SLOTS, found[0], picks, extra)
+        return low + ROUND_SLOTS, found
+
+    _, found = lax.while_loop(lambda state: state[0] < most, more, (window, found))
     return found[1], found[2].reshape(8), found[3].reshape(8)
 
 
 def solution(mesh):
-    torus = Mesh(mesh.devices.reshape(NYH, NY0, NZH, NZ0, NC, NX), NAMES)
+    torus = Mesh(mesh.devices.reshape(NYH, NY0, 2, 2, NZ0, NC, NX), NAMES)
     return jax.shard_map(
         per_device,
         mesh=torus,

time: 93.8 us -> 99.9 us (1.065)
  blocking collectives: 0 us -> 18.5 us
  starting transfers between devices: 53.4 us -> 42.5 us
    all_gather x0 -> x1, blocking collectives: none -> 18.5 us  [per_device(): lax.all_gather(jnp.stack(weights), 'z1').reshape(NZH, *w_first.shape)]
    ppermute x4 -> x2, starting transfers between devices: 25.5 us -> 10.4 us  [per_device(): weights.append(lax.ppermute(w_first, ('yh', 'z2', 'x'), swap))]
    all_to_all x4, starting transfers between devices: 27.9 us -> 32.1 us  [exchange(): return lax.all_to_all(pieces, axes, split_axis=0, concat_axis=0, tiled=True)]
    ppermute x4 -> x2, waiting for transfers between devices: 2.43 us -> 1.97 us  [per_device(): weights.append(lax.ppermute(w_first, ('yh', 'z2', 'x'), swap))]
  transfers between devices with their start and end apart: 8 -> 6, of which waited for: 5 -> 4; matrix products, arithmetic and copies ran while one was open for 4% -> 3% of each run, Pallas kernels for 3% -> 0%
where the time goes in v4:
time: 99.9 us; the launch traced here: 99.4 us
  starting transfers between devices  42.5 us (43%)
  waiting for transfers between devices  24.8 us (25%)
  blocking collectives  18.5 us (19%)
  Pallas kernels  6.65 us (7%)
  other arithmetic  2.25 us (2%)
  local copies, waits for them, and re-layouts  2.12 us (2%)
  between operations  1.99 us (2%)
    all_to_all x4, starting transfers between devices, exchange(): return lax.all_to_all(pieces, axes, split_axis=0, concat_axis=0, tiled=True)  32.1 us
    all_to_all x4, waiting for transfers between devices, exchange(): return lax.all_to_all(pieces, axes, split_axis=0, concat_axis=0, tiled=True)  22.9 us
    all_gather x1, blocking collectives, per_device(): lax.all_gather(jnp.stack(weights), 'z1').reshape(NZH, *w_first.shape)  18.5 us
    ppermute x2, starting transfers between devices, per_device(): weights.append(lax.ppermute(w_first, ('yh', 'z2', 'x'), swap))  10.4 us
    pallas_call x5, Pallas kernels, call(): pl.pallas_call(kernel, out_shape=shapes, in_specs=[SMEM] * scalars + [VME...  6.65 us
  transfers between devices with their start and end apart: 6, of which 4 were waited for; matrix products, arithmetic and copies ran while one was open for 3% of the time, Pallas kernels for 0%

profile of v4, /device:TPU:1, one launch (start us, length us, event | category | flops | bytes accessed | tf_op | source)
XLA Modules:
  0.0 99.4 jit_solution(1873814345246606509)
XLA Ops:
  0.6 0.0 copy-start
  0.7 0.7 copy-done
  1.3 0.0 copy-start.1
  1.3 0.7 copy-done.1
  2.0 2.6 %first_pick_kernel.1 = (bf16[32,16,128]{2,1,0:T(8,128)(2,1)}, f32[2,8,128]{2,1,0:T(8,128)S(1)}) custom-call(s32[2]{0:T(128)S(1)} %call_exported.0.round_ref, s32[8,64]{1,0:T(8,128)} %boundary_ref.3, s32[8,64]{1,0:T(8,128)} %valid_ref.5, bf16[8,64,896]{2,1,0:T(8,128)(2,1)} %hidden_ref.1, f32[8,128]{1,0:T(8,128)S(1)} %bitcast.9, f32[8,128]{1,0:T(8,128)S(1)} %bitcast.10), custom_call_target="tpu_custom_call" | custom-call | tf_op jit(solution)/shard_map/first_pick_kernel/pallas_call | solution.py:167
  4.6 0.0 copy-start.6
  4.6 0.0 copy-start.5
  4.6 10.7 %all-to-all-start.4 = ((bf16[32,16,128]{2,1,0:T(8,128)(2,1)}), bf16[32,16,128]{2,1,0:T(8,128)(2,1)S(1)}, u32[]{:S(2)}, u32[]{:S(2)}) async-start(bf16[32,16,128]{2,1,0:T(8,128)(2,1)} %get-tuple-element.164), calls=%async_computation.4 | async-start | bytes 262144 | tf_op jit(solution)/shard_map/all_to_all | solution.py:182
  15.3 0.0 copy-done.6
  15.3 9.7 %collective-permute-start.1 = (bf16[28,1024]{1,0:T(8,128)(2,1)S(1)}, bf16[28,1024]{1,0:T(8,128)(2,1)S(1)}, u32[]{:S(2)}, u32[]{:S(2)}) collective-permute-start(bf16[28,1024]{1,0:T(8,128)(2,1)S(1)} %copy-done.6), channel_id=1, source_target_pairs={{0,32},{1,160},{2,288},{3,416},{32,0},{33,128},{34,256},{35,384},{... | collective-permute-start | bytes 172040 | tf_op jit(solution)/shard_map/ppermute | solution.py:193
  25.0 0.7 collective-permute-start
  25.7 0.0 copy-done.5
  25.7 0.1 copy.15.pairs_ref
  25.8 2.0 %collective-permute-done.1 = bf16[28,1024]{1,0:T(8,128)(2,1)S(1)} collective-permute-done((bf16[28,1024]{1,0:T(8,128)(2,1)S(1)}, bf16[28,1024]{1,0:T(8,128)(2,1)S(1)}, u32[]{:S(2)}, u32[]{:S(2)}) %collective-permute-start.1) | collective-permute-done | bytes 57376 | tf_op jit(solution)/shard_map/ppermute | solution.py:193
  27.8 0.0 collective-permute-done
  27.8 0.0 copy-start.3
  27.8 0.0 copy-start.4
  27.8 18.5 %all-gather.weight_ref = bf16[4,28,1024]{2,1,0:T(8,128)(2,1)S(1)} all-gather(bf16[2,28,1024]{2,1,0:T(8,128)(2,1)S(1)} %pad_maximum_fusion), channel_id=2, replica_groups=mesh['yh'=4,'y0'=2,'z2'=2,'z1'=2,'z0'=2,'c'=2,'x'=4] {'z1'}, dimensions={0}, use_global_device_ids=true | all-gather | bytes 344064 | tf_op jit(solution)/shard_map/all_gather | solution.py:194
  46.3 0.0 all-to-all-done.4.picks_ref
  46.3 0.0 copy-done.3
  46.3 0.0 copy-done.4
  46.3 1.9 %layer_kernel.5 = f32[32,32,128]{2,1,0:T(8,128)} custom-call(s32[2]{0:T(128)S(1)} %call_exported.0.round_ref, s32[8,64]{1,0:T(8,128)S(1)} %copy-done.4, s32[8,64]{1,0:T(8,128)S(1)} %copy-done.3, bf16[32,16,128]{2,1,0:T(8,128)(2,1)S(1)} %all-to-all-done.4.picks_ref, f32[2,8,128]{2,1,0:T(8,128)S(1)} %get-tuple-element.355.extra_ref, ...), custom_call_target="tpu_custom_call" | custom-call | tf_op jit(solution)/shard_map/layer_kernel/pallas_call | solution.py:167
  48.2 0.1 eq.134
  48.3 0.1 eq.138
  48.4 0.0 copy-start.2
  48.4 9.9 %all-to-all-start.5 = ((f32[32,32,128]{2,1,0:T(8,128)}), f32[32,32,128]{2,1,0:T(8,128)S(1)}, u32[]{:S(2)}, u32[]{:S(2)}) async-start(f32[32,32,128]{2,1,0:T(8,128)} %layer_kernel.5), calls=%async_computation.5 | async-start | bytes 1048576 | tf_op jit(solution)/shard_map/all_to_all | solution.py:182
  58.3 0.5 convert_reduce_fusion.3
  58.8 0.1 add.78
  58.9 0.6 select_reduce_fusion
  60.0 0.6 reduce_max.19
  61.3 0.5 convert_reduce_fusion.2
  61.8 7.6 %all-to-all-done.5.pre_ref = f32[32,32,128]{2,1,0:T(8,128)S(1)} async-done(((f32[32,32,128]{2,1,0:T(8,128)}), f32[32,32,128]{2,1,0:T(8,128)S(1)}, u32[]{:S(2)}, u32[]{:S(2)}) %all-to-all-start.5) | async-done | bytes 524320 | tf_op jit(solution)/shard_map/all_to_all | solution.py:182
  69.4 0.8 head_kernel.5
  70.2 4.3 %all-to-all-start.6 = ((f32[16,1,128]{2,1,0:T(1,128)}), f32[16,1,128]{2,1,0:T(1,128)S(1)}, u32[]{:S(2)}, u32[]{:S(2)}) async-start(f32[16,1,128]{2,1,0:T(1,128)} %head_kernel.5), calls=%async_computation.6 | async-start | bytes 16384 | tf_op jit(solution)/shard_map/all_to_all | solution.py:182
  74.6 0.1 div.24
  74.6 0.1 rem.46
  74.7 0.1 ne.65
  74.8 0.1 lt.106
  74.9 0.1 ge.33
  75.0 6.6 %all-to-all-done.6.share_ref = f32[16,1,128]{2,1,0:T(1,128)S(1)} async-done(((f32[16,1,128]{2,1,0:T(1,128)}), f32[16,1,128]{2,1,0:T(1,128)S(1)}, u32[]{:S(2)}, u32[]{:S(2)}) %all-to-all-start.6) | async-done | bytes 8224 | tf_op jit(solution)/shard_map/all_to_all | solution.py:182
  81.6 0.6 spread_kernel.5
  82.2 7.1 %all-to-all-start.7 = ((f32[32,1,128]{2,1,0:T(1,128)}), f32[32,1,128]{2,1,0:T(1,128)S(1)}, u32[]{:S(2)}, u32[]{:S(2)}) async-start(f32[32,1,128]{2,1,0:T(1,128)} %spread_kernel.5), calls=%async_computation.7 | async-start | bytes 32768 | tf_op jit(solution)/shard_map/all_to_all | solution.py:182
  89.4 8.6 %all-to-all-done.7.share_ref = f32[32,1,128]{2,1,0:T(1,128)S(1)} async-done(((f32[32,1,128]{2,1,0:T(1,128)}), f32[32,1,128]{2,1,0:T(1,128)S(1)}, u32[]{:S(2)}, u32[]{:S(2)}) %all-to-all-start.7) | async-done | bytes 16416 | tf_op jit(solution)/shard_map/all_to_all | solution.py:182
  98.0 0.8 finish_kernel.5
  98.8 0.0 copy-done.2
  98.8 0.6 while.18
  (12 shorter events, 0.1 us)
Async XLA Ops:
  0.6 0.7 copy-start
  1.3 0.7 copy-start.1
  4.6 10.7 %copy-start.6 = (bf16[28,1024]{1,0:T(8,128)(2,1)S(1)}, bf16[28,1024]{1,0:T(8,128)(2,1)}, u32[]{:S(2)}) copy-start(bf16[28,1024]{1,0:T(8,128)(2,1)} %param.14) | copy-start | bytes 172036
  4.6 21.1 %copy-start.5 = (s32[8,2]{0,1:T(2,128)S(1)}, s32[8,2]{0,1:T(2,128)}, u32[]{:S(2)}) copy-start(s32[8,2]{0,1:T(2,128)} %param.13) | copy-start | bytes 196
  4.6 41.7 %all-to-all-start.4 = ((bf16[32,16,128]{2,1,0:T(8,128)(2,1)}), bf16[32,16,128]{2,1,0:T(8,128)(2,1)S(1)}, u32[]{:S(2)}, u32[]{:S(2)}) async-start(bf16[32,16,128]{2,1,0:T(8,128)(2,1)} %get-tuple-element.164), calls=%async_computation.4 | async-start | bytes 262144 | tf_op jit(solution)/shard_map/all_to_all | solution.py:182
  15.3 12.5 %collective-permute-start.1 = (bf16[28,1024]{1,0:T(8,128)(2,1)S(1)}, bf16[28,1024]{1,0:T(8,128)(2,1)S(1)}, u32[]{:S(2)}, u32[]{:S(2)}) collective-permute-start(bf16[28,1024]{1,0:T(8,128)(2,1)S(1)} %copy-done.6), channel_id=1, source_target_pairs={{0,32},{1,160},{2,288},{3,416},{32,0},{33,128},{34,256},{35,384},{... | collective-permute-start | bytes 172040 | tf_op jit(solution)/shard_map/ppermute | solution.py:193
  25.0 2.7 %collective-permute-start = (bf16[28,1024]{1,0:T(8,128)(2,1)S(1)}, bf16[28,1024]{1,0:T(8,128)(2,1)S(1)}, u32[]{:S(2)}, u32[]{:S(2)}) collective-permute-start(bf16[28,1024]{1,0:T(8,128)(2,1)S(1)} %copy-done.6), channel_id=1, source_target_pairs={{0,0},{1,128},{2,256},{3,384},{32,32},{33,160},{34,288},{35,416},{... | collective-permute-start | bytes 172040 | tf_op jit(solution)/shard_map/ppermute | solution.py:193
  27.8 18.5 %copy-start.3 = (s32[8,64]{1,0:T(8,128)S(1)}, s32[8,64]{1,0:T(8,128)}, u32[]{:S(2)}) copy-start(s32[8,64]{1,0:T(8,128)} %valid_ref.5) | copy-start | bytes 6148
  27.8 18.5 %copy-start.4 = (s32[8,64]{1,0:T(8,128)S(1)}, s32[8,64]{1,0:T(8,128)}, u32[]{:S(2)}) copy-start(s32[8,64]{1,0:T(8,128)} %boundary_ref.3) | copy-start | bytes 6148
  48.4 50.4 %copy-start.2 = (bf16[8,64,896]{2,1,0:T(8,128)(2,1)S(1)}, bf16[8,64,896]{2,1,0:T(8,128)(2,1)}, u32[]{:S(2)}) copy-start(bf16[8,64,896]{2,1,0:T(8,128)(2,1)} %hidden_ref.1) | copy-start | bytes 2752516
  48.4 21.1 %all-to-all-start.5 = ((f32[32,32,128]{2,1,0:T(8,128)}), f32[32,32,128]{2,1,0:T(8,128)S(1)}, u32[]{:S(2)}, u32[]{:S(2)}) async-start(f32[32,32,128]{2,1,0:T(8,128)} %layer_kernel.5), calls=%async_computation.5 | async-start | bytes 1048576 | tf_op jit(solution)/shard_map/all_to_all | solution.py:182
  70.2 11.4 %all-to-all-start.6 = ((f32[16,1,128]{2,1,0:T(1,128)}), f32[16,1,128]{2,1,0:T(1,128)S(1)}, u32[]{:S(2)}, u32[]{:S(2)}) async-start(f32[16,1,128]{2,1,0:T(1,128)} %head_kernel.5), calls=%async_computation.6 | async-start | bytes 16384 | tf_op jit(solution)/shard_map/all_to_all | solution.py:182
  82.2 15.8 %all-to-all-start.7 = ((f32[32,1,128]{2,1,0:T(1,128)}), f32[32,1,128]{2,1,0:T(1,128)S(1)}, u32[]{:S(2)}, u32[]{:S(2)}) async-start(f32[32,1,128]{2,1,0:T(1,128)} %spread_kernel.5), calls=%async_computation.7 | async-start | bytes 32768 | tf_op jit(solution)/shard_map/all_to_all | solution.py:182

commit v5 on v4

--- a/solution.py
+++ b/solution.py
@@ -35,13 +35,20 @@
     return (owner >> 2) & 3
 
 
-def first_pick_kernel(round_ref, boundary_ref, valid_ref, hidden_ref, bias_ref, second_ref, out_ref, extra_ref):
-    extra_ref[0] = bias_ref[...]
-    extra_ref[1] = second_ref[...]
-    pick_kernel(round_ref, boundary_ref, valid_ref, hidden_ref, out_ref)
-
-
-def pick_kernel(round_ref, boundary_ref, valid_ref, hidden_ref, out_ref):
+def first_pick_kernel(
+    round_ref, boundary_ref, valid_ref, far_ref, bias_ref, second_ref, out_ref, extra_ref, hidden_ref, sems
+):
+    copies = [
+        pltpu.make_async_copy(bias_ref, extra_ref.at[0], sems.at[1]),
+        pltpu.make_async_copy(second_ref, extra_ref.at[1], sems.at[2]),
+    ]
+    pick_kernel(round_ref, boundary_ref, valid_ref, far_ref, out_ref, hidden_ref, sems, copies)
+
+
+def pick_kernel(round_ref, boundary_ref, valid_ref, far_ref, out_ref, hidden_ref, sems, others=()):
+    copies = [pltpu.make_async_copy(far_ref, hidden_ref, sems.at[0]), *others]
+    for copy in copies:
+        copy.start()
     me, low = lax.axis_index(SEQ), round_ref[0]
     traces, steps = boundary_ref.shape
     tokens = hidden_ref.shape[1]
@@ -54,12 +61,16 @@
     earlier = ones_where(iota((traces, traces), 1) < iota((traces, traces), 0), BF16)
     carried = jnp.dot(earlier, totals.astype(BF16), preferred_element_type=F32)
     slot = jnp.where(mine, (within + carried).astype(I32) - low, -1)
-    picked = jnp.zeros((SLOTS, hidden_ref.shape[2]), F32)
+    chosen = []
     for t in range(traces):
         hit = slot[t : t + 1, :] == iota((SLOTS, steps), 0)
         token = jnp.sum(jnp.where(hit, local[t : t + 1, :] + 1, 0).astype(F32), axis=1, keepdims=True)
-        choose = ones_where(token.astype(I32) == iota((SLOTS, tokens), 1) + 1, BF16)
-        picked += jnp.dot(choose, hidden_ref[t], preferred_element_type=F32)
+        chosen.append(ones_where(token.astype(I32) == iota((SLOTS, tokens), 1) + 1, BF16))
+    for copy in copies:
+        copy.wait()
+    picked = jnp.zeros((SLOTS, hidden_ref.shape[2]), F32)
+    for t in range(traces):
+        picked += jnp.dot(chosen[t], hidden_ref[t], preferred_element_type=F32)
     depth = hidden_ref.shape[2] // (BLOCKS * NZH)
     pad = jnp.zeros((SLOTS, DEEP - depth), F32)
     for y0 in range(NY0):
@@ -162,15 +173,16 @@
     margin_ref[...] = jnp.sum(jnp.where(diagonal, ends[0] - ends[1], 0.0), axis=0, keepdims=True)
 
 
-def call(kernel, shapes, *args, scalars=0):
+def call(kernel, shapes, *args, scalars=0, far=0, scratch=()):
     single = not isinstance(shapes, list)
+    near = len(args) - scalars - far
     return pl.pallas_call(
         kernel,
         out_shape=shapes,
-        in_specs=[SMEM] * scalars + [VMEM] * (len(args) - scalars),
+        in_specs=[SMEM] * scalars + [VMEM] * near + [pl.BlockSpec(memory_space=pl.ANY)] * far,
         out_specs=VMEM if single else [VMEM] * len(shapes),
+        scratch_shapes=scratch,
         compiler_params=pltpu.CompilerParams(vmem_limit_bytes=16 << 20),
-        name=kernel.__name__,
     )(*args)
 
 
@@ -202,12 +214,13 @@
         rank = jnp.sum(same & (order[None, :] < order[:, None]), axis=1, dtype=I32)
         return owner, live, rank, group_of(owner)
 
-    def limits(owner, live, rank, group):
+    def limits(live, rank, group):
         most = jnp.max(jnp.where(live, rank + 1, 0))
         crowd = jnp.max(jnp.sum((group[:, None] == group[None, :]) & live[None, :], axis=1, dtype=I32))
         return most, jnp.where((most <= SLOTS) & (crowd <= CAP), SLOTS, ROUND_SLOTS).astype(I32)
 
     shape = array((OWNERS, SLOTS, 128), BF16)
+    scratch = (pltpu.VMEM(hidden_states.shape, BF16), pltpu.SemaphoreType.DMA((3,)))
 
     def one_round(numbers, low, window, before, picks, extra):
         most = None
@@ -219,7 +232,7 @@
         pre, late_boundary, late_valid = lax.optimization_barrier((pre, boundary, valid))
         owner, live, rank, group = ranks(late_boundary, late_valid)
         if window is None:
-            most, window = limits(owner, live, rank, group)
+            most, window = limits(live, rank, group)
         pre = exchange(pre, ("x", "y0", "z0", "c"))
         share = exchange(call(head_kernel, array((NYH * NY0 * NC, 1, 128)), pre), ("yh", "y0", "c"))
         share = call(spread_kernel, array((NZH * NX * NZ0, 1, 128)), share)
@@ -239,14 +252,16 @@
     first = jnp.array([0, 0], I32)
     picks, extra = call(
         first_pick_kernel, [shape, array((2, 8, 128))],
-        first, boundary, valid, hidden_states, bias, second, scalars=1,
+        first, boundary, valid, hidden_states, bias, second, scalars=1, far=3, scratch=scratch,
     )
     found, most, window = one_round(first, 0, None, jnp.zeros(boundary.shape, F32), picks, extra)
 
     def more(state):
         low, found = state
         numbers = jnp.stack([low, jnp.int32(ROUND_SLOTS)])
-        picks = call(pick_kernel, shape, numbers, boundary, valid, hidden_states, scalars=1)
+        picks = call(
+            pick_kernel, shape, numbers, boundary, valid, hidden_states, scalars=1, far=1, scratch=scratch
+        )
         found, _, _ = one_round(numbers, low, ROUND_SLOTS, found[0], picks, extra)
         return low + ROUND_SLOTS, found
 

time: 99.9 us -> 100 us (level)
  no operation moved by 1% of the time
where the time goes in v5:
time: 100 us; the launch traced here: 99.8 us
  starting transfers between devices  42.5 us (42%)
  waiting for transfers between devices  24.8 us (25%)
  blocking collectives  18.5 us (18%)
  Pallas kernels  7.01 us (7%)
  other arithmetic  2.25 us (2%)
  local copies, waits for them, and re-layouts  2.12 us (2%)
  between operations  2.01 us (2%)
    all_to_all x4, starting transfers between devices, exchange(): return lax.all_to_all(pieces, axes, split_axis=0, concat_axis=0, tiled=True)  32.1 us
    all_to_all x4, waiting for transfers between devices, exchange(): return lax.all_to_all(pieces, axes, split_axis=0, concat_axis=0, tiled=True)  22.9 us
    all_gather x1, blocking collectives, per_device(): lax.all_gather(jnp.stack(weights), 'z1').reshape(NZH, *w_first.shape)  18.5 us
    ppermute x2, starting transfers between devices, per_device(): weights.append(lax.ppermute(w_first, ('yh', 'z2', 'x'), swap))  10.4 us
    pallas_call x5, Pallas kernels, call(): pl.pallas_call(kernel, out_shape=shapes, in_specs=[SMEM] * scalars + [VME...  7.01 us
  transfers between devices with their start and end apart: 6, of which 4 were waited for; matrix products, arithmetic and copies ran while one was open for 3% of the time, Pallas kernels for 0%

profile of v5, /device:TPU:1, one launch (start us, length us, event | category | flops | bytes accessed | tf_op | source)
XLA Modules:
  0.0 99.8 jit_solution(9970681326013141674)
XLA Ops:
  0.6 0.0 copy-start
  0.7 0.7 copy-done
  1.3 0.0 copy-start.1
  1.3 0.7 copy-done.1
  2.0 2.9 %shard_map.103 = (bf16[32,16,128]{2,1,0:T(8,128)(2,1)}, f32[2,8,128]{2,1,0:T(8,128)S(1)}) custom-call(s32[2]{0:T(128)S(1)} %call_exported.0.round_ref, s32[8,64]{1,0:T(8,128)} %boundary_ref.3, s32[8,64]{1,0:T(8,128)} %valid_ref.5, bf16[8,64,896]{2,1,0:T(8,128)(2,1)} %far_ref.1, f32[8,128]{1,0:T(8,128)S(1)} %bitcast.9, f32[8,128]{1,0:T(8,128)S(1)} %bitcast.10), custom_call_target="tpu_custom_call" | custom-call | tf_op jit(solution)/shard_map/pallas_call | solution.py:179
  4.9 0.0 copy-start.6
  5.0 0.0 copy-start.5
  5.0 10.7 %all-to-all-start.4 = ((bf16[32,16,128]{2,1,0:T(8,128)(2,1)}), bf16[32,16,128]{2,1,0:T(8,128)(2,1)S(1)}, u32[]{:S(2)}, u32[]{:S(2)}) async-start(bf16[32,16,128]{2,1,0:T(8,128)(2,1)} %get-tuple-element.164), calls=%async_computation.4 | async-start | bytes 262144 | tf_op jit(solution)/shard_map/all_to_all | solution.py:194
  15.7 0.0 copy-done.6
  15.7 9.7 %collective-permute-start.1 = (bf16[28,1024]{1,0:T(8,128)(2,1)S(1)}, bf16[28,1024]{1,0:T(8,128)(2,1)S(1)}, u32[]{:S(2)}, u32[]{:S(2)}) collective-permute-start(bf16[28,1024]{1,0:T(8,128)(2,1)S(1)} %copy-done.6), channel_id=1, source_target_pairs={{0,32},{1,160},{2,288},{3,416},{32,0},{33,128},{34,256},{35,384},{... | collective-permute-start | bytes 172040 | tf_op jit(solution)/shard_map/ppermute | solution.py:205
  25.4 0.7 collective-permute-start
  26.1 0.0 copy-done.5
  26.1 0.1 copy.15.pairs_ref
  26.2 2.0 %collective-permute-done.1 = bf16[28,1024]{1,0:T(8,128)(2,1)S(1)} collective-permute-done((bf16[28,1024]{1,0:T(8,128)(2,1)S(1)}, bf16[28,1024]{1,0:T(8,128)(2,1)S(1)}, u32[]{:S(2)}, u32[]{:S(2)}) %collective-permute-start.1) | collective-permute-done | bytes 57376 | tf_op jit(solution)/shard_map/ppermute | solution.py:205
  28.2 0.0 collective-permute-done
  28.2 0.0 copy-start.3
  28.2 0.0 copy-start.4
  28.2 18.5 %all-gather.weight_ref = bf16[4,28,1024]{2,1,0:T(8,128)(2,1)S(1)} all-gather(bf16[2,28,1024]{2,1,0:T(8,128)(2,1)S(1)} %pad_maximum_fusion), channel_id=2, replica_groups=mesh['yh'=4,'y0'=2,'z2'=2,'z1'=2,'z0'=2,'c'=2,'x'=4] {'z1'}, dimensions={0}, use_global_device_ids=true | all-gather | bytes 344064 | tf_op jit(solution)/shard_map/all_gather | solution.py:206
  46.7 0.0 all-to-all-done.4.picks_ref
  46.7 0.0 copy-done.3
  46.7 0.0 copy-done.4
  46.7 1.9 %shard_map.104 = f32[32,32,128]{2,1,0:T(8,128)} custom-call(s32[2]{0:T(128)S(1)} %call_exported.0.round_ref, s32[8,64]{1,0:T(8,128)S(1)} %copy-done.4, s32[8,64]{1,0:T(8,128)S(1)} %copy-done.3, bf16[32,16,128]{2,1,0:T(8,128)(2,1)S(1)} %all-to-all-done.4.picks_ref, f32[2,8,128]{2,1,0:T(8,128)S(1)} %get-tuple-element.355.extra_ref, ...), custom_call_target="tpu_custom_call" | custom-call | tf_op jit(solution)/shard_map/pallas_call | solution.py:179
  48.6 0.1 eq.134
  48.7 0.1 eq.138
  48.8 0.0 copy-start.2
  48.8 9.9 %all-to-all-start.5 = ((f32[32,32,128]{2,1,0:T(8,128)}), f32[32,32,128]{2,1,0:T(8,128)S(1)}, u32[]{:S(2)}, u32[]{:S(2)}) async-start(f32[32,32,128]{2,1,0:T(8,128)} %shard_map.104), calls=%async_computation.5 | async-start | bytes 1048576 | tf_op jit(solution)/shard_map/all_to_all | solution.py:194
  58.7 0.5 convert_reduce_fusion.3
  59.2 0.1 add.78
  59.3 0.6 select_reduce_fusion
  60.4 0.6 reduce_max.19
  61.7 0.5 convert_reduce_fusion.2
  62.2 7.6 %all-to-all-done.5.pre_ref = f32[32,32,128]{2,1,0:T(8,128)S(1)} async-done(((f32[32,32,128]{2,1,0:T(8,128)}), f32[32,32,128]{2,1,0:T(8,128)S(1)}, u32[]{:S(2)}, u32[]{:S(2)}) %all-to-all-start.5) | async-done | bytes 524320 | tf_op jit(solution)/shard_map/all_to_all | solution.py:194
  69.8 0.8 shard_map.105
  70.6 4.3 %all-to-all-start.6 = ((f32[16,1,128]{2,1,0:T(1,128)}), f32[16,1,128]{2,1,0:T(1,128)S(1)}, u32[]{:S(2)}, u32[]{:S(2)}) async-start(f32[16,1,128]{2,1,0:T(1,128)} %shard_map.105), calls=%async_computation.6 | async-start | bytes 16384 | tf_op jit(solution)/shard_map/all_to_all | solution.py:194
  75.0 0.1 div.24
  75.0 0.1 rem.46
  75.1 0.1 ne.65
  75.2 0.1 lt.106
  75.3 0.1 ge.33
  75.4 6.6 %all-to-all-done.6.share_ref = f32[16,1,128]{2,1,0:T(1,128)S(1)} async-done(((f32[16,1,128]{2,1,0:T(1,128)}), f32[16,1,128]{2,1,0:T(1,128)S(1)}, u32[]{:S(2)}, u32[]{:S(2)}) %all-to-all-start.6) | async-done | bytes 8224 | tf_op jit(solution)/shard_map/all_to_all | solution.py:194
  82.0 0.6 shard_map.106
  82.6 7.1 %all-to-all-start.7 = ((f32[32,1,128]{2,1,0:T(1,128)}), f32[32,1,128]{2,1,0:T(1,128)S(1)}, u32[]{:S(2)}, u32[]{:S(2)}) async-start(f32[32,1,128]{2,1,0:T(1,128)} %shard_map.106), calls=%async_computation.7 | async-start | bytes 32768 | tf_op jit(solution)/shard_map/all_to_all | solution.py:194
  89.8 8.6 %all-to-all-done.7.share_ref = f32[32,1,128]{2,1,0:T(1,128)S(1)} async-done(((f32[32,1,128]{2,1,0:T(1,128)}), f32[32,1,128]{2,1,0:T(1,128)S(1)}, u32[]{:S(2)}, u32[]{:S(2)}) %all-to-all-start.7) | async-done | bytes 16416 | tf_op jit(solution)/shard_map/all_to_all | solution.py:194
  98.4 0.8 shard_map.107
  99.2 0.0 copy-done.2
  99.2 0.6 while.18
  (12 shorter events, 0.1 us)
Async XLA Ops:
  0.6 0.7 copy-start
  1.3 0.7 copy-start.1
  4.9 10.7 %copy-start.6 = (bf16[28,1024]{1,0:T(8,128)(2,1)S(1)}, bf16[28,1024]{1,0:T(8,128)(2,1)}, u32[]{:S(2)}) copy-start(bf16[28,1024]{1,0:T(8,128)(2,1)} %param.14) | copy-start | bytes 172036
  5.0 21.2 %copy-start.5 = (s32[8,2]{0,1:T(2,128)S(1)}, s32[8,2]{0,1:T(2,128)}, u32[]{:S(2)}) copy-start(s32[8,2]{0,1:T(2,128)} %param.13) | copy-start | bytes 196
  5.0 41.7 %all-to-all-start.4 = ((bf16[32,16,128]{2,1,0:T(8,128)(2,1)}), bf16[32,16,128]{2,1,0:T(8,128)(2,1)S(1)}, u32[]{:S(2)}, u32[]{:S(2)}) async-start(bf16[32,16,128]{2,1,0:T(8,128)(2,1)} %get-tuple-element.164), calls=%async_computation.4 | async-start | bytes 262144 | tf_op jit(solution)/shard_map/all_to_all | solution.py:194
  15.7 12.5 %collective-permute-start.1 = (bf16[28,1024]{1,0:T(8,128)(2,1)S(1)}, bf16[28,1024]{1,0:T(8,128)(2,1)S(1)}, u32[]{:S(2)}, u32[]{:S(2)}) collective-permute-start(bf16[28,1024]{1,0:T(8,128)(2,1)S(1)} %copy-done.6), channel_id=1, source_target_pairs={{0,32},{1,160},{2,288},{3,416},{32,0},{33,128},{34,256},{35,384},{... | collective-permute-start | bytes 172040 | tf_op jit(solution)/shard_map/ppermute | solution.py:205
  25.4 2.7 %collective-permute-start = (bf16[28,1024]{1,0:T(8,128)(2,1)S(1)}, bf16[28,1024]{1,0:T(8,128)(2,1)S(1)}, u32[]{:S(2)}, u32[]{:S(2)}) collective-permute-start(bf16[28,1024]{1,0:T(8,128)(2,1)S(1)} %copy-done.6), channel_id=1, source_target_pairs={{0,0},{1,128},{2,256},{3,384},{32,32},{33,160},{34,288},{35,416},{... | collective-permute-start | bytes 172040 | tf_op jit(solution)/shard_map/ppermute | solution.py:205
  28.2 18.5 %copy-start.3 = (s32[8,64]{1,0:T(8,128)S(1)}, s32[8,64]{1,0:T(8,128)}, u32[]{:S(2)}) copy-start(s32[8,64]{1,0:T(8,128)} %valid_ref.5) | copy-start | bytes 6148
  28.2 18.5 %copy-start.4 = (s32[8,64]{1,0:T(8,128)S(1)}, s32[8,64]{1,0:T(8,128)}, u32[]{:S(2)}) copy-start(s32[8,64]{1,0:T(8,128)} %boundary_ref.3) | copy-start | bytes 6148
  48.8 50.4 %copy-start.2 = (bf16[8,64,896]{2,1,0:T(8,128)(2,1)S(1)}, bf16[8,64,896]{2,1,0:T(8,128)(2,1)}, u32[]{:S(2)}) copy-start(bf16[8,64,896]{2,1,0:T(8,128)(2,1)} %far_ref.1) | copy-start | bytes 2752516
  48.8 21.1 %all-to-all-start.5 = ((f32[32,32,128]{2,1,0:T(8,128)}), f32[32,32,128]{2,1,0:T(8,128)S(1)}, u32[]{:S(2)}, u32[]{:S(2)}) async-start(f32[32,32,128]{2,1,0:T(8,128)} %shard_map.104), calls=%async_computation.5 | async-start | bytes 1048576 | tf_op jit(solution)/shard_map/all_to_all | solution.py:194
  70.6 11.4 %all-to-all-start.6 = ((f32[16,1,128]{2,1,0:T(1,128)}), f32[16,1,128]{2,1,0:T(1,128)S(1)}, u32[]{:S(2)}, u32[]{:S(2)}) async-start(f32[16,1,128]{2,1,0:T(1,128)} %shard_map.105), calls=%async_computation.6 | async-start | bytes 16384 | tf_op jit(solution)/shard_map/all_to_all | solution.py:194
  82.6 15.8 %all-to-all-start.7 = ((f32[32,1,128]{2,1,0:T(1,128)}), f32[32,1,128]{2,1,0:T(1,128)S(1)}, u32[]{:S(2)}, u32[]{:S(2)}) async-start(f32[32,1,128]{2,1,0:T(1,128)} %shard_map.106), calls=%async_computation.7 | async-start | bytes 32768 | tf_op jit(solution)/shard_map/all_to_all | solution.py:194

commit v6 on v5

--- a/solution.py
+++ b/solution.py
@@ -35,23 +35,32 @@
     return (owner >> 2) & 3
 
 
-def first_pick_kernel(
-    round_ref, boundary_ref, valid_ref, far_ref, bias_ref, second_ref, out_ref, extra_ref, hidden_ref, sems
+def first_pick_kernel(round_ref, *refs):
+    ends, bias_ref, second_ref, out_ref, extra_ref, *scratch = refs[:3], *refs[3:]
+    sems = scratch[-1]
+    copies = [
+        pltpu.make_async_copy(bias_ref, extra_ref.at[0], sems.at[3]),
+        pltpu.make_async_copy(second_ref, extra_ref.at[1], sems.at[4]),
+    ]
+    pick_kernel(round_ref, *ends, out_ref, *scratch, others=copies)
+
+
+def pick_kernel(
+    round_ref, far_boundary, far_valid, far_hidden, out_ref, boundary_ref, valid_ref, hidden_ref, sems, others=()
 ):
     copies = [
-        pltpu.make_async_copy(bias_ref, extra_ref.at[0], sems.at[1]),
-        pltpu.make_async_copy(second_ref, extra_ref.at[1], sems.at[2]),
+        pltpu.make_async_copy(far_boundary, boundary_ref, sems.at[0]),
+        pltpu.make_async_copy(far_valid, valid_ref, sems.at[1]),
+        pltpu.make_async_copy(far_hidden, hidden_ref, sems.at[2]),
+        *others,
     ]
-    pick_kernel(round_ref, boundary_ref, valid_ref, far_ref, out_ref, hidden_ref, sems, copies)
-
-
-def pick_kernel(round_ref, boundary_ref, valid_ref, far_ref, out_ref, hidden_ref, sems, others=()):
-    copies = [pltpu.make_async_copy(far_ref, hidden_ref, sems.at[0]), *others]
     for copy in copies:
         copy.start()
     me, low = lax.axis_index(SEQ), round_ref[0]
     traces, steps = boundary_ref.shape
     tokens = hidden_ref.shape[1]
+    for copy in copies[:2]:
+        copy.wait()
     local = boundary_ref[...] - me * tokens
     mine = (local >= 0) & (local < tokens) & (valid_ref[...] == 1)
     owned = ones_where(mine, BF16)
@@ -66,7 +75,7 @@
         hit = slot[t : t + 1, :] == iota((SLOTS, steps), 0)
         token = jnp.sum(jnp.where(hit, local[t : t + 1, :] + 1, 0).astype(F32), axis=1, keepdims=True)
         chosen.append(ones_where(token.astype(I32) == iota((SLOTS, tokens), 1) + 1, BF16))
-    for copy in copies:
+    for copy in copies[2:]:
         copy.wait()
     picked = jnp.zeros((SLOTS, hidden_ref.shape[2]), F32)
     for t in range(traces):
@@ -116,7 +125,7 @@
     pad = jnp.zeros((DEEP - weight_ref.shape[1], weight_ref.shape[2]), BF16)
     weight = []
     for source in range(NZH):
-        weight += [weight_ref[(source & 1) * 2 + ((source >> 1) ^ (zh >> 1))], pad]
+        weight += [weight_ref[source], pad]
     partial = jnp.dot(rows.astype(BF16), jnp.concatenate(weight, axis=0), preferred_element_type=F32)
     for x in range(NX):
         for j in range(BLOCKS):
@@ -165,12 +174,12 @@
     diagonal = iota((traces, traces), 0) == iota((traces, traces), 1)
     flat = jnp.sum(jnp.where(diagonal, score, 0.0), axis=0, keepdims=True)
     score_ref[...] = flat
-    trace = iota((traces, traces), 1)
+    trace = iota((traces, traces), 0)
     pairs = pairs_ref[...]
     ends = []
     for e in range(2):
-        ends.append(jnp.sum(jnp.where(pairs[:, e : e + 1] == trace, flat, 0.0), axis=1, keepdims=True))
-    margin_ref[...] = jnp.sum(jnp.where(diagonal, ends[0] - ends[1], 0.0), axis=0, keepdims=True)
+        ends.append(jnp.sum(jnp.where(pairs[e : e + 1, :] == trace, score, 0.0), axis=0, keepdims=True))
+    margin_ref[...] = ends[0] - ends[1]
 
 
 def call(kernel, shapes, *args, scalars=0, far=0, scratch=()):
@@ -179,7 +188,7 @@
     return pl.pallas_call(
         kernel,
         out_shape=shapes,
-        in_specs=[SMEM] * scalars + [VMEM] * near + [pl.BlockSpec(memory_space=pl.ANY)] * far,
+        in_specs=[SMEM] * scalars + [VMEM] * near + [pl.BlockSpec(memory_space=pltpu.HBM)] * far,
         out_specs=VMEM if single else [VMEM] * len(shapes),
         scratch_shapes=scratch,
         compiler_params=pltpu.CompilerParams(vmem_limit_bytes=16 << 20),
@@ -196,14 +205,9 @@
 
 def per_device(hidden_states, boundary, valid, pairs, w_first, b_first, w_second):
     columns = w_first.shape[1]
-    weights = []
-    for flip in range(2):
-        swap = []
-        for a in range(NYH):
-            for z in range(2):
-                swap += [((a * 2 + z) * NX + b, (b * 2 + (z ^ flip)) * NX + a) for b in range(NX)]
-        weights.append(lax.ppermute(w_first, ("yh", "z2", "x"), swap))
-    weight = lax.all_gather(jnp.stack(weights), "z1").reshape(NZH, *w_first.shape)
+    swap = [(a * NX + b, b * NX + a) for a in range(NYH) for b in range(NX)]
+    weight = lax.ppermute(w_first, ("yh", "x"), swap)
+    weight = lax.all_gather(weight, ZH)
     bias, second = b_first.reshape(8, columns // 8), w_second.reshape(8, columns // 8)
 
     def ranks(boundary, valid):
@@ -220,7 +224,10 @@
         return most, jnp.where((most <= SLOTS) & (crowd <= CAP), SLOTS, ROUND_SLOTS).astype(I32)
 
     shape = array((OWNERS, SLOTS, 128), BF16)
-    scratch = (pltpu.VMEM(hidden_states.shape, BF16), pltpu.SemaphoreType.DMA((3,)))
+    scratch = (
+        pltpu.VMEM(boundary.shape, I32), pltpu.VMEM(valid.shape, I32), pltpu.VMEM(hidden_states.shape, BF16),
+        pltpu.SemaphoreType.DMA((5,)),
+    )
 
     def one_round(numbers, low, window, before, picks, extra):
         most = None
@@ -229,30 +236,32 @@
             layer_kernel, array((NX * BLOCKS, DEEP, 128)),
             numbers, boundary, valid, picks, extra, weight, scalars=1,
         )
-        pre, late_boundary, late_valid = lax.optimization_barrier((pre, boundary, valid))
+        pre, late_boundary, late_valid, late_pairs = lax.optimization_barrier((pre, boundary, valid, pairs))
+        pre = exchange(pre, ("x", "y0", "z0", "c"))
         owner, live, rank, group = ranks(late_boundary, late_valid)
         if window is None:
             most, window = limits(live, rank, group)
-        pre = exchange(pre, ("x", "y0", "z0", "c"))
-        share = exchange(call(head_kernel, array((NYH * NY0 * NC, 1, 128)), pre), ("yh", "y0", "c"))
-        share = call(spread_kernel, array((NZH * NX * NZ0, 1, 128)), share)
-        share = exchange(share, ZH + ("x", "z0"))
         inside = live & (rank >= low) & (rank < low + window)
         ahead = inside[None, :] & (group[None, :] == group[:, None]) & (owner[None, :] < owner[:, None])
         g = jnp.sum(ahead, axis=1, dtype=I32) + rank - low
         place = (group * NX + g // PART) * 128 + g % PART
         place = jnp.where(inside, place, -128).reshape(boundary.shape)
         place = jnp.pad(place, ((0, 0), (0, 128 - boundary.shape[1])), constant_values=-128)
+        chosen = before, late_valid, jnp.pad(late_pairs.T, ((0, 6), (0, 0)))
+        pre, place, chosen = lax.optimization_barrier((pre, place, chosen))
+        share = exchange(call(head_kernel, array((NYH * NY0 * NC, 1, 128)), pre), ("yh", "y0", "c"))
+        share = call(spread_kernel, array((NZH * NX * NZ0, 1, 128)), share)
+        share = exchange(share, ZH + ("x", "z0"))
         found = call(
             finish_kernel, [array(boundary.shape), array(boundary.shape), array((1, 8)), array((1, 8))],
-            share, place, before, valid, pairs,
+            share, place, *chosen,
         )
         return found, most, window
 
     first = jnp.array([0, 0], I32)
     picks, extra = call(
         first_pick_kernel, [shape, array((2, 8, 128))],
-        first, boundary, valid, hidden_states, bias, second, scalars=1, far=3, scratch=scratch,
+        first, boundary, valid, hidden_states, bias, second, scalars=1, far=5, scratch=scratch,
     )
     found, most, window = one_round(first, 0, None, jnp.zeros(boundary.shape, F32), picks, extra)
 
@@ -260,7 +269,7 @@
         low, found = state
         numbers = jnp.stack([low, jnp.int32(ROUND_SLOTS)])
         picks = call(
-            pick_kernel, shape, numbers, boundary, valid, hidden_states, scalars=1, far=1, scratch=scratch
+            pick_kernel, shape, numbers, boundary, valid, hidden_states, scalars=1, far=3, scratch=scratch
         )
         found, _, _ = one_round(numbers, low, ROUND_SLOTS, found[0], picks, extra)
         return low + ROUND_SLOTS, found

time: 100 us -> 97.6 us (0.976)
  blocking collectives: 18.5 us -> 41.4 us
  waiting for transfers between devices: 24.8 us -> 9.48 us
  starting transfers between devices: 42.5 us -> 32.8 us
  Pallas kernels: 7.01 us -> 5.6 us
    all_to_all x0 -> x2, blocking collectives: none -> 24.6 us  [exchange(): return lax.all_to_all(pieces, axes, split_axis=0, concat_axis=0, tiled=True)]
    all_to_all x4 -> x2, waiting for transfers between devices: 22.9 us -> 9.48 us  [exchange(): return lax.all_to_all(pieces, axes, split_axis=0, concat_axis=0, tiled=True)]
    ppermute x2 -> x1, starting transfers between devices: 10.4 us -> 0.66 us  [per_device(): weight = lax.ppermute(w_first, ('yh', 'x'), swap)]
    ppermute x2 -> x1, waiting for transfers between devices: 1.97 us -> 0.01 us  [per_device(): weight = lax.ppermute(w_first, ('yh', 'x'), swap)]
    all_gather x1, blocking collectives: 18.5 us -> 16.8 us  [per_device(): weight = lax.all_gather(weight, ZH)]
    pallas_call x5, Pallas kernels: 7.01 us -> 5.6 us  [call(): pl.pallas_call(kernel, out_shape=shapes, in_specs=[SMEM] * scalars + [VME...]
    unnamed x15 -> x14, local copies, waits for them, and re-layouts: 1.47 us -> 2.06 us
    all_to_all x4 -> x2, starting transfers between devices: 32.1 us -> 32.2 us  [exchange(): return lax.all_to_all(pieces, axes, split_axis=0, concat_axis=0, tiled=True)]
  transfers between devices with their start and end apart: 6 -> 3, of which waited for: 4 -> 1; matrix products, arithmetic and copies ran while one was open for 3% -> 1% of each run, Pallas kernels for 0% -> 0%
where the time goes in v6:
time: 97.6 us; the launch traced here: 97.1 us
  blocking collectives  41.4 us (42%)
  starting transfers between devices  32.8 us (34%)
  waiting for transfers between devices  9.48 us (10%)
  Pallas kernels  5.6 us (6%)
  local copies, waits for them, and re-layouts  2.73 us (3%)
  other arithmetic  2.27 us (2%)
  between operations  2.08 us (2%)
    all_to_all x2, starting transfers between devices, exchange(): return lax.all_to_all(pieces, axes, split_axis=0, concat_axis=0, tiled=True)  32.2 us
    all_to_all x2, blocking collectives, exchange(): return lax.all_to_all(pieces, axes, split_axis=0, concat_axis=0, tiled=True)  24.6 us
    all_gather x1, blocking collectives, per_device(): weight = lax.all_gather(weight, ZH)  16.8 us
    all_to_all x2, waiting for transfers between devices, exchange(): return lax.all_to_all(pieces, axes, split_axis=0, concat_axis=0, tiled=True)  9.48 us
    pallas_call x5, Pallas kernels, call(): pl.pallas_call(kernel, out_shape=shapes, in_specs=[SMEM] * scalars + [VME...  5.6 us
    unnamed x14, local copies, waits for them, and re-layouts  2.06 us
  transfers between devices with their start and end apart: 3, of which 1 were waited for; matrix products, arithmetic and copies ran while one was open for 1% of the time, Pallas kernels for 0%

profile of v6, /device:TPU:1, one launch (start us, length us, event | category | flops | bytes accessed | tf_op | source)
XLA Modules:
  0.0 97.1 jit_solution(17518659964792452423)
XLA Ops:
  0.6 0.0 copy-start
  0.7 0.7 copy-done
  1.3 0.0 copy-start.1
  1.3 0.7 copy-done.1
  2.0 2.8 %shard_map.103 = (bf16[32,16,128]{2,1,0:T(8,128)(2,1)}, f32[2,8,128]{2,1,0:T(8,128)S(1)}) custom-call(s32[2]{0:T(128)S(1)} %call_exported.0.round_ref, s32[8,64]{1,0:T(8,128)} %boundary_ref.1, s32[8,64]{1,0:T(8,128)} %valid_ref.2, bf16[8,64,896]{2,1,0:T(8,128)(2,1)} %refs_2_.1, f32[8,128]{1,0:T(8,128)S(1)} %bitcast.12, f32[8,128]{1,0:T(8,128)S(1)} %bitcast.13), custom_call_target="tpu_custom_call" | custom-call | tf_op jit(solution)/shard_map/pallas_call | solution.py:188
  4.8 0.0 copy-start.6
  4.8 10.7 %all-to-all-start.4 = ((bf16[32,16,128]{2,1,0:T(8,128)(2,1)}), bf16[32,16,128]{2,1,0:T(8,128)(2,1)S(1)}, u32[]{:S(2)}, u32[]{:S(2)}) async-start(bf16[32,16,128]{2,1,0:T(8,128)(2,1)} %get-tuple-element.179), calls=%async_computation.4 | async-start | bytes 262144 | tf_op jit(solution)/shard_map/all_to_all | solution.py:203
  15.5 0.0 copy-done.6
  15.6 0.7 collective-permute-start
  16.2 0.0 collective-permute-done
  16.2 0.0 copy-start.3
  16.2 0.0 copy-start.4
  16.3 16.8 %all-gather.1.weight_ref = bf16[4,28,1024]{2,1,0:T(8,128)(2,1)S(1)} all-gather(bf16[1,28,1024]{2,1,0:T(8,128)(2,1)S(1)} %bitcast.14), channel_id=2, replica_groups=mesh['yh'=4,'y0'=2,'z2'=2,'z1'=2,'z0'=2,'c'=2,'x'=4] {'z2','z1'}, dimensions={0}, use_global_device_ids=true | all-gather | bytes 286720 | tf_op jit(solution)/shard_map/all_gather | solution.py:210
  33.1 0.0 all-to-all-done.4.picks_ref
  33.1 0.0 copy-done.3
  33.1 0.0 copy-done.4
  33.1 1.9 %shard_map.104 = f32[32,32,128]{2,1,0:T(8,128)} custom-call(s32[2]{0:T(128)S(1)} %call_exported.0.round_ref, s32[8,64]{1,0:T(8,128)S(1)} %copy-done.4, s32[8,64]{1,0:T(8,128)S(1)} %copy-done.3, bf16[32,16,128]{2,1,0:T(8,128)(2,1)S(1)} %all-to-all-done.4.picks_ref, f32[2,8,128]{2,1,0:T(8,128)S(1)} %get-tuple-element.352.extra_ref, ...), custom_call_target="tpu_custom_call" | custom-call | tf_op jit(solution)/shard_map/pallas_call | solution.py:188
  35.0 0.1 eq.134
  35.1 0.1 eq.138
  35.2 0.5 convert_reduce_fusion.3
  35.6 0.0 copy-start.2
  35.6 0.1 add.82
  35.7 0.6 select_reduce_fusion
  37.0 0.6 reduce_max.19
  38.3 21.5 %all-to-all-start.5 = ((f32[32,32,128]{2,1,0:T(8,128)}), f32[32,32,128]{2,1,0:T(8,128)S(1)}, u32[]{:S(2)}, u32[]{:S(2)}) async-start(f32[32,32,128]{2,1,0:T(8,128)} %shard_map.104), calls=%async_computation.5 | async-start | bytes 1048576 | tf_op jit(solution)/shard_map/all_to_all | solution.py:203
  59.8 0.5 convert_reduce_fusion.2
  60.3 0.1 div.24
  60.4 0.1 rem.46
  60.4 0.1 ne.65
  60.5 0.1 lt.106
  60.6 0.1 ge.33
  60.7 0.0 copy-start.5
  60.7 0.7 copy-done.5
  61.4 9.5 %all-to-all-done.5.pre_ref = f32[32,32,128]{2,1,0:T(8,128)S(1)} async-done(((f32[32,32,128]{2,1,0:T(8,128)}), f32[32,32,128]{2,1,0:T(8,128)S(1)}, u32[]{:S(2)}, u32[]{:S(2)}) %all-to-all-start.5) | async-done | bytes 524320 | tf_op jit(solution)/shard_map/all_to_all | solution.py:203
  70.9 0.2 shard_map.105
  71.1 11.1 %all_to_all.47.share_ref = f32[16,1,128]{2,1,0:T(1,128)S(1)} all-to-all(f32[16,1,128]{2,1,0:T(1,128)S(1)} %shard_map.105), channel_id=1, replica_groups=mesh['yh'=4,'y0'=2,'z2'=2,'z1'=2,'z0'=2,'c'=2,'x'=4] {'yh','y0','c'}, dimensions={0} | all-to-all | bytes 16384 | tf_op jit(solution)/shard_map/all_to_all | solution.py:203
  82.2 13.6 %all_to_all.48.share_ref = f32[32,1,128]{2,1,0:T(1,128)S(1)} all-to-all(f32[32,1,128]{2,1,0:T(1,128)S(1)} %shard_map.106), channel_id=1, replica_groups=mesh['yh'=4,'y0'=2,'z2'=2,'z1'=2,'z0'=2,'c'=2,'x'=4] {'z2','z1','x','z0'}, dimensions={0} | all-to-all | bytes 32768 | tf_op jit(solution)/shard_map/all_to_all | solution.py:203
  95.7 0.7 shard_map.107
  96.4 0.0 copy-done.2
  96.4 0.6 while.18
  (13 shorter events, 0.1 us)
Async XLA Ops:
  0.6 0.7 copy-start
  1.3 0.7 copy-start.1
  4.8 10.7 %copy-start.6 = (bf16[28,1024]{1,0:T(8,128)(2,1)S(1)}, bf16[28,1024]{1,0:T(8,128)(2,1)}, u32[]{:S(2)}) copy-start(bf16[28,1024]{1,0:T(8,128)(2,1)} %param.14) | copy-start | bytes 172036
  4.8 28.2 %all-to-all-start.4 = ((bf16[32,16,128]{2,1,0:T(8,128)(2,1)}), bf16[32,16,128]{2,1,0:T(8,128)(2,1)S(1)}, u32[]{:S(2)}, u32[]{:S(2)}) async-start(bf16[32,16,128]{2,1,0:T(8,128)(2,1)} %get-tuple-element.179), calls=%async_computation.4 | async-start | bytes 262144 | tf_op jit(solution)/shard_map/all_to_all | solution.py:203
  15.6 0.7 collective-permute-start
  16.2 16.8 %copy-start.3 = (s32[8,64]{1,0:T(8,128)S(1)}, s32[8,64]{1,0:T(8,128)}, u32[]{:S(2)}) copy-start(s32[8,64]{1,0:T(8,128)} %valid_ref.2) | copy-start | bytes 6148
  16.2 16.8 %copy-start.4 = (s32[8,64]{1,0:T(8,128)S(1)}, s32[8,64]{1,0:T(8,128)}, u32[]{:S(2)}) copy-start(s32[8,64]{1,0:T(8,128)} %boundary_ref.1) | copy-start | bytes 6148
  35.6 60.8 %copy-start.2 = (bf16[8,64,896]{2,1,0:T(8,128)(2,1)S(1)}, bf16[8,64,896]{2,1,0:T(8,128)(2,1)}, u32[]{:S(2)}) copy-start(bf16[8,64,896]{2,1,0:T(8,128)(2,1)} %refs_2_.1) | copy-start | bytes 2752516
  38.3 32.6 %all-to-all-start.5 = ((f32[32,32,128]{2,1,0:T(8,128)}), f32[32,32,128]{2,1,0:T(8,128)S(1)}, u32[]{:S(2)}, u32[]{:S(2)}) async-start(f32[32,32,128]{2,1,0:T(8,128)} %shard_map.104), calls=%async_computation.5 | async-start | bytes 1048576 | tf_op jit(solution)/shard_map/all_to_all | solution.py:203
  60.7 0.7 copy-start.5

commit v7 on v6

--- a/solution.py
+++ b/solution.py
@@ -36,13 +36,14 @@
 
 
 def first_pick_kernel(round_ref, *refs):
-    ends, bias_ref, second_ref, out_ref, extra_ref, *scratch = refs[:3], *refs[3:]
+    inputs, bias_ref, second_ref, pairs_ref, out_ref, extra_ref, ends_ref, *scratch = refs[:3], *refs[3:]
     sems = scratch[-1]
     copies = [
         pltpu.make_async_copy(bias_ref, extra_ref.at[0], sems.at[3]),
         pltpu.make_async_copy(second_ref, extra_ref.at[1], sems.at[4]),
+        pltpu.make_async_copy(pairs_ref, ends_ref, sems.at[5]),
     ]
-    pick_kernel(round_ref, *ends, out_ref, *scratch, others=copies)
+    pick_kernel(round_ref, *inputs, out_ref, *scratch, others=copies)
 
 
 def pick_kernel(
@@ -77,9 +78,8 @@
         chosen.append(ones_where(token.astype(I32) == iota((SLOTS, tokens), 1) + 1, BF16))
     for copy in copies[2:]:
         copy.wait()
-    picked = jnp.zeros((SLOTS, hidden_ref.shape[2]), F32)
-    for t in range(traces):
-        picked += jnp.dot(chosen[t], hidden_ref[t], preferred_element_type=F32)
+    hidden = hidden_ref[...].reshape(traces * tokens, hidden_ref.shape[2])
+    picked = jnp.dot(jnp.concatenate(chosen, axis=1), hidden, preferred_element_type=F32)
     depth = hidden_ref.shape[2] // (BLOCKS * NZH)
     pad = jnp.zeros((SLOTS, DEEP - depth), F32)
     for y0 in range(NY0):
@@ -93,34 +93,53 @@
                 out_ref[yh * BLOCKS + y0 * 4 + low2] = piece
 
 
-def layer_kernel(round_ref, boundary_ref, valid_ref, picks_ref, extra_ref, weight_ref, out_ref):
+def layer_kernel(
+    round_ref, boundary_ref, valid_ref, picks_ref, extra_ref, weight_ref, out_ref, place_ref, low_ref, most_ref
+):
     low, window = round_ref[0], round_ref[1]
     traces, steps = boundary_ref.shape
+    pad = jnp.full((traces, 128 - steps), -1, I32)
     owner = jnp.where(valid_ref[...] == 1, boundary_ref[...] >> 6, -1)
-    count = jnp.zeros((128, steps), F32)
-    for t in range(traces):
-        count += ones_where(owner[t : t + 1, :] == iota((128, steps), 0))
-    count = jnp.sum(count, axis=1, keepdims=True)
-    device = iota((128, 1), 0)
-    most = jnp.max(count, axis=0, keepdims=True)
+    lane = iota((traces, 128), 1)
+    count = jnp.zeros((traces, 128), F32)
+    for k in range(steps):
+        count += ones_where(owner[:, k : k + 1] == lane)
+    row, column = iota((128, 128), 0), iota((128, 128), 1)
+    less = jnp.dot(count.astype(BF16), ones_where(row < column, BF16), preferred_element_type=F32)
+    earlier = ones_where(iota((traces, traces), 1) < iota((traces, traces), 0), BF16)
+    carried = jnp.dot(earlier, count.astype(BF16), preferred_element_type=F32)
+    total = jnp.broadcast_to(jnp.sum(count, axis=0, keepdims=True), count.shape)
+    most = jnp.max(total, axis=1, keepdims=True)
     fits = most <= SLOTS
     for group in range(NZH):
-        crowd = jnp.sum(jnp.where(group_of(device) == group, count, 0.0), axis=0, keepdims=True)
+        crowd = jnp.sum(jnp.where(group_of(lane) == group, total, 0.0), axis=1, keepdims=True)
         fits = fits & (crowd <= CAP)
     top = jnp.where(window > 0, window.astype(F32), jnp.where(fits, float(SLOTS), float(ROUND_SLOTS)))
-    count = jnp.clip(count - low.astype(F32), 0.0, top)
+    most_ref[0] = most.astype(I32)[0, 0]
+    low_ref[0] = low + top.astype(I32)[0, 0]
+    taken = jnp.clip(total - low.astype(F32), 0.0, top)
+    ahead = ones_where((row < column) & (group_of(row) == group_of(column)), BF16)
+    start = jnp.dot(taken.astype(BF16), ahead, preferred_element_type=F32)
+
+    where = jnp.concatenate([owner, pad], axis=1)
+    index = jnp.maximum(where, 0)
+    rank = jnp.take_along_axis(carried - less, index, axis=1) + lane.astype(F32) - low.astype(F32)
+    g = (jnp.take_along_axis(start, index, axis=1) + rank).astype(I32)
+    part = (g >= PART).astype(I32) + (g >= 2 * PART).astype(I32) + (g >= 3 * PART).astype(I32)
+    place = (group_of(index) * NX + part) * 128 + g - PART * part
+    place_ref[...] = jnp.where((where >= 0) & (rank >= 0.0) & (rank < top), place, -128)
+
     zh = lax.axis_index(ZH)
-    mine = group_of(device) == zh
-    count = jnp.where(mine, count, 0.0)
-    place_in_group = (device >> 4) * 4 + (device & 3)
-    lane = iota((128, OWNERS * SLOTS), 1) >> 4
-    number = jnp.sum(jnp.where(lane == place_in_group, count, 0.0), axis=0, keepdims=True).astype(I32)
-    start = jnp.sum(jnp.where(lane > place_in_group, count, 0.0), axis=0, keepdims=True).astype(I32)
-    slot = iota((1, OWNERS * SLOTS), 1) & (SLOTS - 1)
-    g = start + slot
-    g = g + 2 * ((g >= PART).astype(I32) + (g >= 2 * PART).astype(I32) + (g >= 3 * PART).astype(I32))
-    g = jnp.where(slot < number, g, -1)
-    choose = ones_where(g == iota((NX * DEEP, OWNERS * SLOTS), 0), BF16)
+    slot = lane & (SLOTS - 1)
+    choices = []
+    for block in range(OWNERS * SLOTS // 128):
+        device = (lane >> 4) + block * 8
+        device = ((device >> 2) << 4) + (zh << 2) + (device & 3)
+        g = jnp.take_along_axis(start, device, axis=1).astype(I32) + slot
+        g = g + 2 * ((g >= PART).astype(I32) + (g >= 2 * PART).astype(I32) + (g >= 3 * PART).astype(I32))
+        g = jnp.where(slot < jnp.take_along_axis(taken, device, axis=1).astype(I32), g, -1)
+        choices.append(ones_where(g[0:1, :] == iota((NX * DEEP, 128), 0), BF16))
+    choose = jnp.concatenate(choices, axis=1)
     rows = jnp.dot(choose, picks_ref[...].reshape(OWNERS * SLOTS, 128), preferred_element_type=F32)
     pad = jnp.zeros((DEEP - weight_ref.shape[1], weight_ref.shape[2]), BF16)
     weight = []
@@ -182,14 +201,14 @@
     margin_ref[...] = ends[0] - ends[1]
 
 
-def call(kernel, shapes, *args, scalars=0, far=0, scratch=()):
+def call(kernel, shapes, *args, scalars=0, far=0, scratch=(), scalars_out=0):
     single = not isinstance(shapes, list)
     near = len(args) - scalars - far
     return pl.pallas_call(
         kernel,
         out_shape=shapes,
         in_specs=[SMEM] * scalars + [VMEM] * near + [pl.BlockSpec(memory_space=pltpu.HBM)] * far,
-        out_specs=VMEM if single else [VMEM] * len(shapes),
+        out_specs=VMEM if single else [VMEM] * (len(shapes) - scalars_out) + [SMEM] * scalars_out,
         scratch_shapes=scratch,
         compiler_params=pltpu.CompilerParams(vmem_limit_bytes=16 << 20),
     )(*args)
@@ -204,66 +223,41 @@
 
 
 def per_device(hidden_states, boundary, valid, pairs, w_first, b_first, w_second):
-    columns = w_first.shape[1]
+    columns, traces = w_first.shape[1], boundary.shape[0]
     swap = [(a * NX + b, b * NX + a) for a in range(NYH) for b in range(NX)]
     weight = lax.ppermute(w_first, ("yh", "x"), swap)
     weight = lax.all_gather(weight, ZH)
     bias, second = b_first.reshape(8, columns // 8), w_second.reshape(8, columns // 8)
 
-    def ranks(boundary, valid):
-        owner = (boundary >> 6).reshape(-1)
-        live = valid.reshape(-1) == 1
-        order = jnp.arange(owner.shape[0], dtype=I32)
-        same = (owner[:, None] == owner[None, :]) & live[None, :]
-        rank = jnp.sum(same & (order[None, :] < order[:, None]), axis=1, dtype=I32)
-        return owner, live, rank, group_of(owner)
-
-    def limits(live, rank, group):
-        most = jnp.max(jnp.where(live, rank + 1, 0))
-        crowd = jnp.max(jnp.sum((group[:, None] == group[None, :]) & live[None, :], axis=1, dtype=I32))
-        return most, jnp.where((most <= SLOTS) & (crowd <= CAP), SLOTS, ROUND_SLOTS).astype(I32)
-
     shape = array((OWNERS, SLOTS, 128), BF16)
     scratch = (
         pltpu.VMEM(boundary.shape, I32), pltpu.VMEM(valid.shape, I32), pltpu.VMEM(hidden_states.shape, BF16),
-        pltpu.SemaphoreType.DMA((5,)),
-    )
-
-    def one_round(numbers, low, window, before, picks, extra):
-        most = None
+        pltpu.SemaphoreType.DMA((6,)),
+    )
+
+    def one_round(numbers, before, picks, extra, ends):
         picks = exchange(picks, ("yh", "y0", "z0", "c"))
-        pre = call(
-            layer_kernel, array((NX * BLOCKS, DEEP, 128)),
-            numbers, boundary, valid, picks, extra, weight, scalars=1,
+        pre, place, low, most = call(
+            layer_kernel,
+            [array((NX * BLOCKS, DEEP, 128)), array((traces, 128), I32)] + [array((1,), I32)] * 2,
+            numbers, boundary, valid, picks, extra, weight, scalars=1, scalars_out=2,
         )
-        pre, late_boundary, late_valid, late_pairs = lax.optimization_barrier((pre, boundary, valid, pairs))
         pre = exchange(pre, ("x", "y0", "z0", "c"))
-        owner, live, rank, group = ranks(late_boundary, late_valid)
-        if window is None:
-            most, window = limits(live, rank, group)
-        inside = live & (rank >= low) & (rank < low + window)
-        ahead = inside[None, :] & (group[None, :] == group[:, None]) & (owner[None, :] < owner[:, None])
-        g = jnp.sum(ahead, axis=1, dtype=I32) + rank - low
-        place = (group * NX + g // PART) * 128 + g % PART
-        place = jnp.where(inside, place, -128).reshape(boundary.shape)
-        place = jnp.pad(place, ((0, 0), (0, 128 - boundary.shape[1])), constant_values=-128)
-        chosen = before, late_valid, jnp.pad(late_pairs.T, ((0, 6), (0, 0)))
-        pre, place, chosen = lax.optimization_barrier((pre, place, chosen))
         share = exchange(call(head_kernel, array((NYH * NY0 * NC, 1, 128)), pre), ("yh", "y0", "c"))
         share = call(spread_kernel, array((NZH * NX * NZ0, 1, 128)), share)
         share = exchange(share, ZH + ("x", "z0"))
         found = call(
             finish_kernel, [array(boundary.shape), array(boundary.shape), array((1, 8)), array((1, 8))],
-            share, place, *chosen,
+            share, place, before, valid, ends,
         )
-        return found, most, window
+        return found, low.reshape(()), most.reshape(())
 
     first = jnp.array([0, 0], I32)
-    picks, extra = call(
-        first_pick_kernel, [shape, array((2, 8, 128))],
-        first, boundary, valid, hidden_states, bias, second, scalars=1, far=5, scratch=scratch,
-    )
-    found, most, window = one_round(first, 0, None, jnp.zeros(boundary.shape, F32), picks, extra)
+    picks, extra, ends = call(
+        first_pick_kernel, [shape, array((2, 8, 128)), array((2, traces), I32)],
+        first, boundary, valid, hidden_states, bias, second, pairs.T, scalars=1, far=6, scratch=scratch,
+    )
+    found, low, most = one_round(first, jnp.zeros(boundary.shape, F32), picks, extra, ends)
 
     def more(state):
         low, found = state
@@ -271,10 +265,10 @@
         picks = call(
             pick_kernel, shape, numbers, boundary, valid, hidden_states, scalars=1, far=3, scratch=scratch
         )
-        found, _, _ = one_round(numbers, low, ROUND_SLOTS, found[0], picks, extra)
-        return low + ROUND_SLOTS, found
-
-    _, found = lax.while_loop(lambda state: state[0] < most, more, (window, found))
+        found, low, _ = one_round(numbers, found[0], picks, extra, ends)
+        return low, found
+
+    _, found = lax.while_loop(lambda state: state[0] < most, more, (low, found))
     return found[1], found[2].reshape(8), found[3].reshape(8)
 
 

time: 97.6 us -> 94.7 us (0.970)
  blocking collectives: 41.4 us -> 73.9 us
  starting transfers between devices: 32.8 us -> 11.4 us
  waiting for transfers between devices: 9.48 us -> 0.01 us
  other arithmetic: 2.27 us -> 0 us
  local copies, waits for them, and re-layouts: 2.73 us -> 1.38 us
  between operations: 2.08 us -> 0.76 us
    all_to_all x2 -> x3, blocking collectives: 24.6 us -> 57.1 us  [exchange(): return lax.all_to_all(pieces, axes, split_axis=0, concat_axis=0, tiled=True)]
    all_to_all x2 -> x1, starting transfers between devices: 32.2 us -> 10.7 us  [exchange(): return lax.all_to_all(pieces, axes, split_axis=0, concat_axis=0, tiled=True)]
    all_to_all x2 -> x1, waiting for transfers between devices: 9.48 us -> 0.01 us  [exchange(): return lax.all_to_all(pieces, axes, split_axis=0, concat_axis=0, tiled=True)]
    reduce_max x2 -> x0, other arithmetic: 1.28 us -> none  [the longest x1 0.65 us: limits(): most = jnp.max(jnp.where(live, rank + 1, 0))]
  transfers between devices with their start and end apart: 3 -> 2, of which waited for: 1 -> 0; matrix products, arithmetic and copies ran while one was open for 1% -> 0% of each run, Pallas kernels for 0% -> 0%
where the time goes in v7:
time: 94.7 us; the launch traced here: 94.2 us
  blocking collectives  73.9 us (78%)
  starting transfers between devices  11.4 us (12%)
  Pallas kernels  5.39 us (6%)
  local copies, waits for them, and re-layouts  1.38 us (1%)
  loops' own time  1.38 us (1%)
    all_to_all x3, blocking collectives, exchange(): return lax.all_to_all(pieces, axes, split_axis=0, concat_axis=0, tiled=True)  57.1 us
    all_gather x1, blocking collectives, per_device(): weight = lax.all_gather(weight, ZH)  16.8 us
    all_to_all x1, starting transfers between devices, exchange(): return lax.all_to_all(pieces, axes, split_axis=0, concat_axis=0, tiled=True)  10.7 us
    pallas_call x5, Pallas kernels, call(): pl.pallas_call(kernel, out_shape=shapes, in_specs=[SMEM] * scalars + [VME...  5.39 us
  transfers between devices with their start and end apart: 2, of which 0 were waited for; matrix products, arithmetic and copies ran while one was open for 0% of the time, Pallas kernels for 0%

profile of v7, /device:TPU:1, one launch (start us, length us, event | category | flops | bytes accessed | tf_op | source)
XLA Modules:
  0.0 94.2 jit_solution(14127873366332163975)
XLA Ops:
  0.6 0.0 copy-start
  0.6 0.0 copy-start.2
  0.7 0.7 copy-done
  1.3 0.0 copy-done.2
  1.3 0.0 copy-start.1
  1.3 0.7 copy-done.1
  2.0 2.8 %shard_map.103 = (bf16[32,16,128]{2,1,0:T(8,128)(2,1)}, f32[2,8,128]{2,1,0:T(8,128)S(1)}, s32[2,8]{1,0:T(2,128)S(1)}) custom-call(s32[2]{0:T(128)S(1)} %call_exported.0.round_ref, s32[8,64]{1,0:T(8,128)} %boundary_ref.1, s32[8,64]{1,0:T(8,128)} %valid_ref.3, bf16[8,64,896]{2,1,0:T(8,128)(2,1)} %refs_2_.1, f32[8,128]{1,0:T(8,128)S(1)} %bitcast.12, ...), custom_call_target="tpu_custom_call" | custom-call | tf_op jit(solution)/shard_map/pallas_call | solution.py:207
  4.9 0.0 copy-start.6
  4.9 10.7 %all-to-all-start.4 = ((bf16[32,16,128]{2,1,0:T(8,128)(2,1)}), bf16[32,16,128]{2,1,0:T(8,128)(2,1)S(1)}, u32[]{:S(2)}, u32[]{:S(2)}) async-start(bf16[32,16,128]{2,1,0:T(8,128)(2,1)} %get-tuple-element.83), calls=%async_computation.4 | async-start | bytes 262144 | tf_op jit(solution)/shard_map/all_to_all | solution.py:222
  15.6 0.0 copy-done.6
  15.6 0.7 collective-permute-start
  16.3 0.0 collective-permute-done
  16.3 0.0 copy-start.4
  16.3 0.0 copy-start.5
  16.3 16.8 %all-gather.1.weight_ref = bf16[4,28,1024]{2,1,0:T(8,128)(2,1)S(1)} all-gather(bf16[1,28,1024]{2,1,0:T(8,128)(2,1)S(1)} %bitcast.15), channel_id=2, replica_groups=mesh['yh'=4,'y0'=2,'z2'=2,'z1'=2,'z0'=2,'c'=2,'x'=4] {'z2','z1'}, dimensions={0}, use_global_device_ids=true | all-gather | bytes 286720 | tf_op jit(solution)/shard_map/all_gather | solution.py:229
  33.1 0.0 all-to-all-done.4.picks_ref
  33.1 0.0 copy-done.4
  33.1 0.0 copy-done.5
  33.1 1.7 %shard_map.104 = (f32[32,32,128]{2,1,0:T(8,128)S(1)}, s32[8,128]{1,0:T(8,128)S(1)}, s32[1]{0:T(128)}, s32[1]{0:T(128)}) custom-call(s32[2]{0:T(128)S(1)} %call_exported.0.round_ref, s32[8,64]{1,0:T(8,128)S(1)} %copy-done.5, s32[8,64]{1,0:T(8,128)S(1)} %copy-done.4, bf16[32,16,128]{2,1,0:T(8,128)(2,1)S(1)} %all-to-all-done.4.picks_ref, ...), custom_call_target="tpu_custom_call" | custom-call | tf_op jit(solution)/shard_map/pallas_call | solution.py:207
  34.8 0.0 copy-start.3
  34.8 32.5 %all_to_all.40.pre_ref = f32[32,32,128]{2,1,0:T(8,128)S(1)} all-to-all(f32[32,32,128]{2,1,0:T(8,128)S(1)} %get-tuple-element.86), channel_id=1, replica_groups=mesh['yh'=4,'y0'=2,'z2'=2,'z1'=2,'z0'=2,'c'=2,'x'=4] {'x','y0','z0','c'}, dimensions={0} | all-to-all | bytes 1048576 | tf_op jit(solution)/shard_map/all_to_all | solution.py:222
  67.3 0.2 shard_map.105
  67.5 11.1 %all_to_all.41.share_ref = f32[16,1,128]{2,1,0:T(1,128)S(1)} all-to-all(f32[16,1,128]{2,1,0:T(1,128)S(1)} %shard_map.105), channel_id=1, replica_groups=mesh['yh'=4,'y0'=2,'z2'=2,'z1'=2,'z0'=2,'c'=2,'x'=4] {'yh','y0','c'}, dimensions={0} | all-to-all | bytes 16384 | tf_op jit(solution)/shard_map/all_to_all | solution.py:222
  78.6 13.6 %all_to_all.42.share_ref = f32[32,1,128]{2,1,0:T(1,128)S(1)} all-to-all(f32[32,1,128]{2,1,0:T(1,128)S(1)} %shard_map.106), channel_id=1, replica_groups=mesh['yh'=4,'y0'=2,'z2'=2,'z1'=2,'z0'=2,'c'=2,'x'=4] {'z2','z1','x','z0'}, dimensions={0} | all-to-all | bytes 32768 | tf_op jit(solution)/shard_map/all_to_all | solution.py:222
  92.2 0.7 shard_map.107
  92.9 0.0 copy-done.3
  92.9 1.4 %while.16 = (s32[]{:T(128)}, f32[8,64]{1,0:T(8,128)S(1)}, f32[8,64]{1,0:T(8,128)}, f32[1,8]{1,0:T(1,128)}, f32[1,8]{1,0:T(1,128)}, /*index=5*/s32[]{:T(128)}, s3...) while((s32[]{:T(128)}, f32[8,64]{1,0:T(8,128)S(1)}, ...), condition=%wide.region_1.0_spmd, body=%wide.region_0.0_spmd | while | flops 3 | bytes 1380513 | solution.py:271
  (3 shorter events, 0.0 us)
Async XLA Ops:
  0.6 0.7 copy-start
  0.6 0.7 copy-start.2
  1.3 0.7 copy-start.1
  4.9 10.7 %copy-start.6 = (bf16[28,1024]{1,0:T(8,128)(2,1)S(1)}, bf16[28,1024]{1,0:T(8,128)(2,1)}, u32[]{:S(2)}) copy-start(bf16[28,1024]{1,0:T(8,128)(2,1)} %param.14) | copy-start | bytes 172036
  4.9 28.2 %all-to-all-start.4 = ((bf16[32,16,128]{2,1,0:T(8,128)(2,1)}), bf16[32,16,128]{2,1,0:T(8,128)(2,1)S(1)}, u32[]{:S(2)}, u32[]{:S(2)}) async-start(bf16[32,16,128]{2,1,0:T(8,128)(2,1)} %get-tuple-element.83), calls=%async_computation.4 | async-start | bytes 262144 | tf_op jit(solution)/shard_map/all_to_all | solution.py:222
  15.6 0.7 collective-permute-start
  16.3 16.8 %copy-start.4 = (s32[8,64]{1,0:T(8,128)S(1)}, s32[8,64]{1,0:T(8,128)}, u32[]{:S(2)}) copy-start(s32[8,64]{1,0:T(8,128)} %valid_ref.3) | copy-start | bytes 6148
  16.3 16.8 %copy-start.5 = (s32[8,64]{1,0:T(8,128)S(1)}, s32[8,64]{1,0:T(8,128)}, u32[]{:S(2)}) copy-start(s32[8,64]{1,0:T(8,128)} %boundary_ref.1) | copy-start | bytes 6148
  34.8 58.1 %copy-start.3 = (bf16[8,64,896]{2,1,0:T(8,128)(2,1)S(1)}, bf16[8,64,896]{2,1,0:T(8,128)(2,1)}, u32[]{:S(2)}) copy-start(bf16[8,64,896]{2,1,0:T(8,128)(2,1)} %refs_2_.1) | copy-start | bytes 2752516

commit v8 on v7

--- a/solution.py
+++ b/solution.py
@@ -36,14 +36,13 @@
 
 
 def first_pick_kernel(round_ref, *refs):
-    inputs, bias_ref, second_ref, pairs_ref, out_ref, extra_ref, ends_ref, *scratch = refs[:3], *refs[3:]
+    ends, bias_ref, second_ref, out_ref, extra_ref, *scratch = refs[:3], *refs[3:]
     sems = scratch[-1]
     copies = [
         pltpu.make_async_copy(bias_ref, extra_ref.at[0], sems.at[3]),
         pltpu.make_async_copy(second_ref, extra_ref.at[1], sems.at[4]),
-        pltpu.make_async_copy(pairs_ref, ends_ref, sems.at[5]),
     ]
-    pick_kernel(round_ref, *inputs, out_ref, *scratch, others=copies)
+    pick_kernel(round_ref, *ends, out_ref, *scratch, others=copies)
 
 
 def pick_kernel(
@@ -232,17 +231,21 @@
     shape = array((OWNERS, SLOTS, 128), BF16)
     scratch = (
         pltpu.VMEM(boundary.shape, I32), pltpu.VMEM(valid.shape, I32), pltpu.VMEM(hidden_states.shape, BF16),
-        pltpu.SemaphoreType.DMA((6,)),
-    )
-
-    def one_round(numbers, before, picks, extra, ends):
+        pltpu.SemaphoreType.DMA((5,)),
+    )
+
+    def one_round(numbers, before, picks, extra):
         picks = exchange(picks, ("yh", "y0", "z0", "c"))
         pre, place, low, most = call(
             layer_kernel,
             [array((NX * BLOCKS, DEEP, 128)), array((traces, 128), I32)] + [array((1,), I32)] * 2,
             numbers, boundary, valid, picks, extra, weight, scalars=1, scalars_out=2,
         )
+        pre, late_pairs = lax.optimization_barrier((pre, pairs))
         pre = exchange(pre, ("x", "y0", "z0", "c"))
+        low, most = jnp.maximum(low.reshape(()), 1), jnp.maximum(most.reshape(()), 0)
+        ends = jnp.pad(late_pairs.T, ((0, 6), (0, 0)))
+        pre, low, most, ends = lax.optimization_barrier((pre, low, most, ends))
         share = exchange(call(head_kernel, array((NYH * NY0 * NC, 1, 128)), pre), ("yh", "y0", "c"))
         share = call(spread_kernel, array((NZH * NX * NZ0, 1, 128)), share)
         share = exchange(share, ZH + ("x", "z0"))
@@ -250,14 +253,14 @@
             finish_kernel, [array(boundary.shape), array(boundary.shape), array((1, 8)), array((1, 8))],
             share, place, before, valid, ends,
         )
-        return found, low.reshape(()), most.reshape(())
+        return found, low, most
 
     first = jnp.array([0, 0], I32)
-    picks, extra, ends = call(
-        first_pick_kernel, [shape, array((2, 8, 128)), array((2, traces), I32)],
-        first, boundary, valid, hidden_states, bias, second, pairs.T, scalars=1, far=6, scratch=scratch,
-    )
-    found, low, most = one_round(first, jnp.zeros(boundary.shape, F32), picks, extra, ends)
+    picks, extra = call(
+        first_pick_kernel, [shape, array((2, 8, 128))],
+        first, boundary, valid, hidden_states, bias, second, scalars=1, far=5, scratch=scratch,
+    )
+    found, low, most = one_round(first, jnp.zeros(boundary.shape, F32), picks, extra)
 
     def more(state):
         low, found = state
@@ -265,7 +268,7 @@
         picks = call(
             pick_kernel, shape, numbers, boundary, valid, hidden_states, scalars=1, far=3, scratch=scratch
         )
-        found, low, _ = one_round(numbers, found[0], picks, extra, ends)
+        found, low, _ = one_round(numbers, found[0], picks, extra)
         return low, found
 
     _, found = lax.while_loop(lambda state: state[0] < most, more, (low, found))

time: 94.7 us -> 94.1 us (level)
  blocking collectives: 73.9 us -> 41.4 us
  starting transfers between devices: 11.4 us -> 33 us
  waiting for transfers between devices: 0.01 us -> 9.13 us
  loops' own time: 1.38 us -> 0.01 us
  between operations: 0.76 us -> 2.07 us
    all_to_all x3 -> x2, blocking collectives: 57.1 us -> 24.6 us  [exchange(): return lax.all_to_all(pieces, axes, split_axis=0, concat_axis=0, tiled=True)]
    all_to_all x1 -> x2, starting transfers between devices: 10.7 us -> 32.3 us  [exchange(): return lax.all_to_all(pieces, axes, split_axis=0, concat_axis=0, tiled=True)]
    all_to_all x1 -> x2, waiting for transfers between devices: 0.01 us -> 9.13 us  [exchange(): return lax.all_to_all(pieces, axes, split_axis=0, concat_axis=0, tiled=True)]
    another operation x1, loops' own time: 1.38 us -> 0.01 us  [per_device(): _, found = lax.while_loop(lambda state: state[0] < most, more, (low, found))]
  transfers between devices with their start and end apart: 2 -> 3, of which waited for: 0 -> 1; matrix products, arithmetic and copies ran while one was open for 0% -> 0% of each run, Pallas kernels for 0% -> 0%
where the time goes in v8:
time: 94.1 us; the launch traced here: 93.5 us
  blocking collectives  41.4 us (44%)
  starting transfers between devices  33 us (35%)
  waiting for transfers between devices  9.13 us (10%)
  Pallas kernels  5.88 us (6%)
  between operations  2.07 us (2%)
  local copies, waits for them, and re-layouts  2.06 us (2%)
    all_to_all x2, starting transfers between devices, exchange(): return lax.all_to_all(pieces, axes, split_axis=0, concat_axis=0, tiled=True)  32.3 us
    all_to_all x2, blocking collectives, exchange(): return lax.all_to_all(pieces, axes, split_axis=0, concat_axis=0, tiled=True)  24.6 us
    all_gather x1, blocking collectives, per_device(): weight = lax.all_gather(weight, ZH)  16.8 us
    all_to_all x2, waiting for transfers between devices, exchange(): return lax.all_to_all(pieces, axes, split_axis=0, concat_axis=0, tiled=True)  9.13 us
    pallas_call x5, Pallas kernels, call(): pl.pallas_call(kernel, out_shape=shapes, in_specs=[SMEM] * scalars + [VME...  5.88 us
    unnamed x14, local copies, waits for them, and re-layouts  2.06 us
  transfers between devices with their start and end apart: 3, of which 1 were waited for; matrix products, arithmetic and copies ran while one was open for 0% of the time, Pallas kernels for 0%

profile of v8, /device:TPU:1, one launch (start us, length us, event | category | flops | bytes accessed | tf_op | source)
XLA Modules:
  0.0 93.5 jit_solution(17393142769697609375)
XLA Ops:
  0.6 0.0 copy-start
  0.7 0.7 copy-done
  1.3 0.0 copy-start.1
  1.3 0.7 copy-done.1
  2.0 2.8 %shard_map.103 = (bf16[32,16,128]{2,1,0:T(8,128)(2,1)}, f32[2,8,128]{2,1,0:T(8,128)S(1)}) custom-call(s32[2]{0:T(128)S(1)} %call_exported.0.round_ref, s32[8,64]{1,0:T(8,128)} %boundary_ref.1, s32[8,64]{1,0:T(8,128)} %valid_ref.3, bf16[8,64,896]{2,1,0:T(8,128)(2,1)} %refs_2_.1, f32[8,128]{1,0:T(8,128)S(1)} %bitcast.17, f32[8,128]{1,0:T(8,128)S(1)} %bitcast.18), custom_call_target="tpu_custom_call" | custom-call | tf_op jit(solution)/shard_map/pallas_call | solution.py:206
  4.8 0.0 copy-start.6
  4.8 10.7 %all-to-all-start.4 = ((bf16[32,16,128]{2,1,0:T(8,128)(2,1)}), bf16[32,16,128]{2,1,0:T(8,128)(2,1)S(1)}, u32[]{:S(2)}, u32[]{:S(2)}) async-start(bf16[32,16,128]{2,1,0:T(8,128)(2,1)} %get-tuple-element.93), calls=%async_computation.4 | async-start | bytes 262144 | tf_op jit(solution)/shard_map/all_to_all | solution.py:221
  15.5 0.0 copy-done.6
  15.6 0.7 collective-permute-start
  16.2 0.0 collective-permute-done
  16.2 0.0 copy-start.3
  16.2 0.0 copy-start.4
  16.3 16.8 %all-gather.1.weight_ref = bf16[4,28,1024]{2,1,0:T(8,128)(2,1)S(1)} all-gather(bf16[1,28,1024]{2,1,0:T(8,128)(2,1)S(1)} %bitcast.19), channel_id=2, replica_groups=mesh['yh'=4,'y0'=2,'z2'=2,'z1'=2,'z0'=2,'c'=2,'x'=4] {'z2','z1'}, dimensions={0}, use_global_device_ids=true | all-gather | bytes 286720 | tf_op jit(solution)/shard_map/all_gather | solution.py:228
  33.1 0.0 all-to-all-done.4.picks_ref
  33.1 0.0 copy-done.3
  33.1 0.0 copy-done.4
  33.1 2.2 %shard_map.104 = (f32[32,32,128]{2,1,0:T(8,128)}, s32[8,128]{1,0:T(8,128)S(1)}, s32[1]{0:T(128)}, s32[1]{0:T(128)}) custom-call(s32[2]{0:T(128)S(1)} %call_exported.0.round_ref, s32[8,64]{1,0:T(8,128)S(1)} %copy-done.4, s32[8,64]{1,0:T(8,128)S(1)} %copy-done.3, bf16[32,16,128]{2,1,0:T(8,128)(2,1)S(1)} %all-to-all-done.4.picks_ref, ...), custom_call_target="tpu_custom_call" | custom-call | tf_op jit(solution)/shard_map/pallas_call | solution.py:206
  35.3 0.0 copy-start.2
  35.3 21.6 %all-to-all-start.5 = ((f32[32,32,128]{2,1,0:T(8,128)}), f32[32,32,128]{2,1,0:T(8,128)S(1)}, u32[]{:S(2)}, u32[]{:S(2)}) async-start(f32[32,32,128]{2,1,0:T(8,128)} %get-tuple-element.96), calls=%async_computation.5 | async-start | bytes 1048576 | tf_op jit(solution)/shard_map/all_to_all | solution.py:221
  56.9 0.0 copy-start.5
  56.9 0.7 copy-done.5
  58.9 9.1 %all-to-all-done.5.pre_ref = f32[32,32,128]{2,1,0:T(8,128)S(1)} async-done(((f32[32,32,128]{2,1,0:T(8,128)}), f32[32,32,128]{2,1,0:T(8,128)S(1)}, u32[]{:S(2)}, u32[]{:S(2)}) %all-to-all-start.5) | async-done | bytes 524320 | tf_op jit(solution)/shard_map/all_to_all | solution.py:221
  68.0 0.2 shard_map.105
  68.2 11.1 %all_to_all.44.share_ref = f32[16,1,128]{2,1,0:T(1,128)S(1)} all-to-all(f32[16,1,128]{2,1,0:T(1,128)S(1)} %shard_map.105), channel_id=1, replica_groups=mesh['yh'=4,'y0'=2,'z2'=2,'z1'=2,'z0'=2,'c'=2,'x'=4] {'yh','y0','c'}, dimensions={0} | all-to-all | bytes 16384 | tf_op jit(solution)/shard_map/all_to_all | solution.py:221
  79.3 13.6 %all_to_all.45.share_ref = f32[32,1,128]{2,1,0:T(1,128)S(1)} all-to-all(f32[32,1,128]{2,1,0:T(1,128)S(1)} %shard_map.106), channel_id=1, replica_groups=mesh['yh'=4,'y0'=2,'z2'=2,'z1'=2,'z0'=2,'c'=2,'x'=4] {'z2','z1','x','z0'}, dimensions={0} | all-to-all | bytes 32768 | tf_op jit(solution)/shard_map/all_to_all | solution.py:221
  92.8 0.7 shard_map.107
  93.5 0.0 copy-done.2
  (5 shorter events, 0.0 us)
Async XLA Ops:
  0.6 0.7 copy-start
  1.3 0.7 copy-start.1
  4.8 10.7 %copy-start.6 = (bf16[28,1024]{1,0:T(8,128)(2,1)S(1)}, bf16[28,1024]{1,0:T(8,128)(2,1)}, u32[]{:S(2)}) copy-start(bf16[28,1024]{1,0:T(8,128)(2,1)} %param.14) | copy-start | bytes 172036
  4.8 28.2 %all-to-all-start.4 = ((bf16[32,16,128]{2,1,0:T(8,128)(2,1)}), bf16[32,16,128]{2,1,0:T(8,128)(2,1)S(1)}, u32[]{:S(2)}, u32[]{:S(2)}) async-start(bf16[32,16,128]{2,1,0:T(8,128)(2,1)} %get-tuple-element.93), calls=%async_computation.4 | async-start | bytes 262144 | tf_op jit(solution)/shard_map/all_to_all | solution.py:221
  15.6 0.7 collective-permute-start
  16.2 16.8 %copy-start.3 = (s32[8,64]{1,0:T(8,128)S(1)}, s32[8,64]{1,0:T(8,128)}, u32[]{:S(2)}) copy-start(s32[8,64]{1,0:T(8,128)} %valid_ref.3) | copy-start | bytes 6148
  16.2 16.8 %copy-start.4 = (s32[8,64]{1,0:T(8,128)S(1)}, s32[8,64]{1,0:T(8,128)}, u32[]{:S(2)}) copy-start(s32[8,64]{1,0:T(8,128)} %boundary_ref.1) | copy-start | bytes 6148
  35.3 58.3 %copy-start.2 = (bf16[8,64,896]{2,1,0:T(8,128)(2,1)S(1)}, bf16[8,64,896]{2,1,0:T(8,128)(2,1)}, u32[]{:S(2)}) copy-start(bf16[8,64,896]{2,1,0:T(8,128)(2,1)} %refs_2_.1) | copy-start | bytes 2752516
  35.3 32.7 %all-to-all-start.5 = ((f32[32,32,128]{2,1,0:T(8,128)}), f32[32,32,128]{2,1,0:T(8,128)S(1)}, u32[]{:S(2)}, u32[]{:S(2)}) async-start(f32[32,32,128]{2,1,0:T(8,128)} %get-tuple-element.96), calls=%async_computation.5 | async-start | bytes 1048576 | tf_op jit(solution)/shard_map/all_to_all | solution.py:221
  56.9 0.7 copy-start.5
